TPU v7x, 32 devices: a 4x4x1 block of a 4x4x8 slice. The times are simulated.
32 devices in a mesh: dp: 1 (over z), tp: 4 (over y), cp: 8 (over x, core).
Axes of the slice: x: 4, y: 4, z: 1, core: 2. Of those that a mesh axis runs over, the one named last changes fastest.
The devices are a block of a 4x4x8 slice.
Arguments:
- hidden: bfloat16 [4096, 3072], P(('dp', 'cp'))
- positions: int32 [4096], P(('dp', 'cp'))
- norm_gain: bfloat16 [3072], replicated
- w_query: bfloat16 [3072, 3072], P(None, 'tp')
- w_key: bfloat16 [3072, 1024], P(None, 'tp')
- w_value: bfloat16 [3072, 1024], P(None, 'tp')
- w_out: bfloat16 [3072, 3072], P('tp')
Outputs:
- output 1: bfloat16 [4096, 3072], P(('dp', 'cp'))
- output 2: bfloat16 [4096, 8, 128], P(('dp', 'cp'), 'tp')
- output 3: bfloat16 [4096, 8, 128], P(('dp', 'cp'), 'tp')
All inputs are finite; a program needn't handle non-finite values.
Results may differ from a plain program's by a relative error of at most 0.00840561.
Values are sent between devices in bfloat16 or wider.
A program may use at most 768 MiB of HBM per device.

v0:
```python
import math
import jax
import jax.numpy as jnp
from jax import lax
from jax.sharding import PartitionSpec as P

HEAD = 128
EPS = 1e-5
LOG_THETA = math.log(1000000.0)
SCORE_SCALE = 1.0 / math.sqrt(HEAD)


def rms_norm(hidden, norm_gain):
    hidden_f = hidden.astype(jnp.float32)
    inv_rms = lax.rsqrt(jnp.mean(hidden_f * hidden_f, axis=-1, keepdims=True) + EPS)
    return (hidden_f * inv_rms * norm_gain.astype(jnp.float32)).astype(jnp.bfloat16)


def rope_tables(positions):
    half_dim = HEAD // 2
    inv_freq = jnp.exp(jnp.arange(half_dim, dtype=jnp.float32) * (-2.0 * LOG_THETA / HEAD))
    angles = positions.astype(jnp.float32)[..., None] * inv_freq
    return jnp.cos(angles), jnp.sin(angles)


def apply_rope(head_vals, cos_t, sin_t):
    half_dim = HEAD // 2
    first_half = head_vals[..., :half_dim]
    second_half = head_vals[..., half_dim:]
    return jnp.concatenate([first_half * cos_t - second_half * sin_t, second_half * cos_t + first_half * sin_t], axis=-1)


def project_heads(hidden, positions, norm_gain, w_query, w_key, w_value):
    row_count = hidden.shape[0]
    kv_local = w_key.shape[1] // HEAD
    group_size = w_query.shape[1] // (HEAD * kv_local)
    normed = rms_norm(hidden, norm_gain)
    cos_t, sin_t = rope_tables(positions)
    q_proj = jnp.dot(normed, w_query, preferred_element_type=jnp.float32).reshape(row_count, kv_local, group_size, HEAD)
    queries = apply_rope(q_proj, cos_t[:, None, None, :], sin_t[:, None, None, :]).astype(jnp.bfloat16)
    k_proj = jnp.dot(normed, w_key, preferred_element_type=jnp.float32).reshape(row_count, kv_local, HEAD)
    k_rope = apply_rope(k_proj, cos_t[:, None, :], sin_t[:, None, :]).astype(jnp.bfloat16)
    v_heads = jnp.dot(normed, w_value, preferred_element_type=jnp.float32).astype(jnp.bfloat16).reshape(row_count, kv_local, HEAD)
    return queries, k_rope, v_heads


def own_block_stats(queries, k_rope, v_heads, positions):
    scores = jnp.einsum('uohf,tof->ohut', queries, k_rope, preferred_element_type=jnp.float32) * SCORE_SCALE
    visible = positions[None, :] <= positions[:, None]
    scores = jnp.where(visible, scores, -jnp.inf)
    run_max = jnp.max(scores, axis=-1)
    weights = jnp.exp(scores - run_max[..., None])
    run_sum = jnp.sum(weights, axis=-1)
    acc_out = jnp.einsum('ohut,tof->ohuf', weights.astype(jnp.bfloat16), v_heads, preferred_element_type=jnp.float32)
    return run_max, run_sum, acc_out


def attend_block(queries, kv_blk, soft_stats):
    run_max, run_sum, acc_out = soft_stats
    scores = jnp.einsum('uohf,tof->ohut', queries, kv_blk[0], preferred_element_type=jnp.float32) * SCORE_SCALE
    new_max = jnp.maximum(run_max, jnp.max(scores, axis=-1))
    rescale = jnp.exp(run_max - new_max)
    weights = jnp.exp(scores - new_max[..., None])
    new_sum = run_sum * rescale + jnp.sum(weights, axis=-1)
    new_acc = acc_out * rescale[..., None] + jnp.einsum('ohut,tof->ohuf', weights.astype(jnp.bfloat16), kv_blk[1], preferred_element_type=jnp.float32)
    return new_max, new_sum, new_acc


def output_sum(hidden, soft_stats, w_out):
    run_max, run_sum, acc_out = soft_stats
    attn_o = (acc_out / run_sum[..., None]).astype(jnp.bfloat16)
    w_out_r = w_out.reshape(acc_out.shape[0], acc_out.shape[1], HEAD, hidden.shape[1])
    part_sum = jnp.einsum('ngte,ngef->tf', attn_o, w_out_r, preferred_element_type=jnp.float32).astype(jnp.bfloat16)
    attn_sum = lax.psum(part_sum, 'tp')
    return (hidden.astype(jnp.float32) + attn_sum.astype(jnp.float32)).astype(jnp.bfloat16)


def solution(mesh):
    blocks = mesh.shape['cp']
    shift_pairs = [(src_idx, (src_idx + 1) % blocks) for src_idx in range(blocks)]
    row_spec = P(('dp', 'cp'), None)
    cache_spec = P(('dp', 'cp'), 'tp', None)
    head_cols = P(None, 'tp')

    def local_block(hidden, positions, norm_gain, w_query, w_key, w_value, w_out):
        my_block = lax.axis_index('cp')
        queries, k_rope, v_heads = project_heads(hidden, positions, norm_gain, w_query, w_key, w_value)
        soft_stats = own_block_stats(queries, k_rope, v_heads, positions)

        def shift_step(step_idx, loop_carry):
            kv_blk, stats_in = loop_carry
            kv_blk = lax.ppermute(kv_blk, 'cp', shift_pairs)

            def take_block(state_in):
                return attend_block(queries, kv_blk, state_in)

            def keep_stats(state_in):
                return state_in

            stats_out = lax.cond(step_idx <= my_block, take_block, keep_stats, stats_in)
            return kv_blk, stats_out

        kv_own = jnp.stack([k_rope, v_heads])
        _, soft_stats = lax.fori_loop(1, blocks, shift_step, (kv_own, soft_stats))
        return output_sum(hidden, soft_stats, w_out), k_rope, v_heads

    return jax.shard_map(local_block, mesh=mesh, in_specs=(row_spec, P(('dp', 'cp')), P(None), head_cols, head_cols, head_cols, P('tp', None)), out_specs=(row_spec, cache_spec, cache_spec), check_vma=False)
```

profile of v0, /device:TPU:102, one launch (start us, length us, event | category | flops | bytes accessed | tf_op | source)
XLA Modules:
  0.0 234.4 jit_solution(17841697734295518902)
XLA Ops:
  8.1 1.4 broadcast_compare_fusion
  10.2 2.6 %fusion.15 = f32[512]{0:T(512)S(1)} fusion(bf16[512,3072]{1,0:T(8,128)(2,1)} %param.11), kind=kLoop, calls=%fused_computation.20 | loop fusion | flops 4718080 | bytes 3147776 | tf_op jit(solution)/shard_map/reduce_sum | solution.py:15
  16.2 5.8 %fusion.34 = f32[512,768]{0,1:T(8,128)S(1)} fusion(bf16[3072,768]{1,0:T(8,128)(2,1)} %param.14, bf16[512,3072]{1,0:T(8,128)(2,1)} %param.11, f32[3072]{0:T(1024)S(1)} %convert_element_type.51, f32[512]{0:T(512)S(1)} %add_rsqrt_fusion), kind=kOutput, calls=%fused_computation.55 | convolution fusion | flops 2422210560 | bytes 9451520 | tf_op jit(solution)/shard_map/dot_general | solution.py:39
  22.0 1.3 fusion.39
  23.3 1.6 copy.47
  24.9 2.8 %copy.48 = f32[512,2,3,64]{3,0,2,1:T(8,128)} copy(f32[512,2,3,64]{0,3,2,1:T(8,128)} %get-tuple-element.186) | data formatting | bytes 1572864
  27.6 3.7 %convolution_convert_fusion = bf16[512,256]{0,1:T(8,128)(2,1)S(1)} fusion(bf16[3072,256]{1,0:T(8,128)(2,1)} %param.16, bf16[512,3072]{1,0:T(8,128)(2,1)} %param.11, f32[3072]{0:T(1024)S(1)} %convert_element_type.51, f32[512]{0:T(512)S(1)} %add_rsqrt_fusion), kind=kOutput, calls=%fused_computation.39 | convolution fusion | flops 811728896 | bytes 4995072 | tf_op jit(solution)/shard_map/dot_general | solution.py:43
  35.5 1.4 fusion.20
  36.9 3.2 %fusion.23 = f32[2,3,512,128]{3,2,1,0:T(8,128)} fusion(bf16[512,2,128,1]{0,2,3,1:T(8,128)(2,1)S(1)} %bitcast.66, f32[2,512,512,3]{2,1,3,0:T(8,128)S(1)} %get-tuple-element.195, f32[2,3,512]{2,1,0:T(4,128)S(1)} %get-tuple-element.253, pred[512,512]{0,1:T(8,128)(4,1)S(1)} %broadcast_compare_fusion), kind=kOutput, calls=%fused_computation.31 | convolution fusion | flops 408944640 | bytes 8400896 | tf_op jit(solution)/shard_map/ohut,tof->ohuf/dot_general | solution.py:54
  42.2 100.2 %while.19 = (s32[]{:T(128)}, bf16[2,512,2,128]{3,1,2,0:T(8,128)(2,1)}, f32[2,3,512]{2,1,0:T(4,128)S(1)}, f32[2,3,512]{2,1,0:T(4,128)S(1)}, f32[2,3,512,128]{3,2,...) while((s32[]{:T(128)}, bf16[2,512,2,128]{3,1,2,0:T(8,128)(2,1)}, ...), condition=%wide.region_8.9_spmd, body=%wide.region_3.8_spmd.sunk | while | flops 818681856 | bytes 39264544 | solution.py:104
  42.2 8.6 %collective-permute-done = bf16[2,512,2,128]{3,1,2,0:T(8,128)(2,1)S(1)} collective-permute-done((bf16[2,512,2,128]{3,1,2,0:T(8,128)(2,1)}, bf16[2,512,2,128]{3,1,2,0:T(8,128)(2,1)S(1)}, u32[]{:S(2)}, u32[]{:S(2)}) %collective-permute-start) | collective-permute-done | bytes 524320 | tf_op jit(solution)/shard_map/while/body/eval_jaxpr/ppermute | solution.py:92
  50.8 5.7 %conditional.2 = ((f32[2,3,512]{2,1,0:T(4,128)S(1)}, f32[2,3,512]{2,1,0:T(4,128)S(1)}, f32[2,3,512,128]{3,2,1,0:T(8,128)})) conditional(s32[]{:T(128)} %convert_element_type.92, (f32[2,3,512]{2,1,0:T(4,128)S(1)}, f32[2,3,512]{2,1,0:T(4,128)S(1)}, f32[2,3,512,128]{3,2,1,0:T(8,128)}) %tuple.51, (bf16[2,512,2,128]{3,1,2,0:T(8,128)(2,1)S(1)}, ...), branch_computations={%region_4.4_spmd, %region_5.7_spmd} | conditional | flops 818681856 | bytes 36118616 | solution.py:100
  53.2 2.1 multiply_add_fusion
  57.4 8.6 %collective-permute-done = bf16[2,512,2,128]{3,1,2,0:T(8,128)(2,1)S(1)} collective-permute-done((bf16[2,512,2,128]{3,1,2,0:T(8,128)(2,1)}, bf16[2,512,2,128]{3,1,2,0:T(8,128)(2,1)S(1)}, u32[]{:S(2)}, u32[]{:S(2)}) %collective-permute-start) | collective-permute-done | bytes 524320 | tf_op jit(solution)/shard_map/while/body/eval_jaxpr/ppermute | solution.py:92
  66.0 5.7 %conditional.2 = ((f32[2,3,512]{2,1,0:T(4,128)S(1)}, f32[2,3,512]{2,1,0:T(4,128)S(1)}, f32[2,3,512,128]{3,2,1,0:T(8,128)})) conditional(s32[]{:T(128)} %convert_element_type.92, (f32[2,3,512]{2,1,0:T(4,128)S(1)}, f32[2,3,512]{2,1,0:T(4,128)S(1)}, f32[2,3,512,128]{3,2,1,0:T(8,128)}) %tuple.51, (bf16[2,512,2,128]{3,1,2,0:T(8,128)(2,1)S(1)}, ...), branch_computations={%region_4.4_spmd, %region_5.7_spmd} | conditional | flops 818681856 | bytes 36118616 | solution.py:100
  68.4 2.1 multiply_add_fusion
  72.5 8.6 %collective-permute-done = bf16[2,512,2,128]{3,1,2,0:T(8,128)(2,1)S(1)} collective-permute-done((bf16[2,512,2,128]{3,1,2,0:T(8,128)(2,1)}, bf16[2,512,2,128]{3,1,2,0:T(8,128)(2,1)S(1)}, u32[]{:S(2)}, u32[]{:S(2)}) %collective-permute-start) | collective-permute-done | bytes 524320 | tf_op jit(solution)/shard_map/while/body/eval_jaxpr/ppermute | solution.py:92
  81.1 5.7 %conditional.2 = ((f32[2,3,512]{2,1,0:T(4,128)S(1)}, f32[2,3,512]{2,1,0:T(4,128)S(1)}, f32[2,3,512,128]{3,2,1,0:T(8,128)})) conditional(s32[]{:T(128)} %convert_element_type.92, (f32[2,3,512]{2,1,0:T(4,128)S(1)}, f32[2,3,512]{2,1,0:T(4,128)S(1)}, f32[2,3,512,128]{3,2,1,0:T(8,128)}) %tuple.51, (bf16[2,512,2,128]{3,1,2,0:T(8,128)(2,1)S(1)}, ...), branch_computations={%region_4.4_spmd, %region_5.7_spmd} | conditional | flops 818681856 | bytes 36118616 | solution.py:100
  83.5 2.1 multiply_add_fusion
  87.6 8.6 %collective-permute-done = bf16[2,512,2,128]{3,1,2,0:T(8,128)(2,1)S(1)} collective-permute-done((bf16[2,512,2,128]{3,1,2,0:T(8,128)(2,1)}, bf16[2,512,2,128]{3,1,2,0:T(8,128)(2,1)S(1)}, u32[]{:S(2)}, u32[]{:S(2)}) %collective-permute-start) | collective-permute-done | bytes 524320 | tf_op jit(solution)/shard_map/while/body/eval_jaxpr/ppermute | solution.py:92
  96.2 5.7 %conditional.2 = ((f32[2,3,512]{2,1,0:T(4,128)S(1)}, f32[2,3,512]{2,1,0:T(4,128)S(1)}, f32[2,3,512,128]{3,2,1,0:T(8,128)})) conditional(s32[]{:T(128)} %convert_element_type.92, (f32[2,3,512]{2,1,0:T(4,128)S(1)}, f32[2,3,512]{2,1,0:T(4,128)S(1)}, f32[2,3,512,128]{3,2,1,0:T(8,128)}) %tuple.51, (bf16[2,512,2,128]{3,1,2,0:T(8,128)(2,1)S(1)}, ...), branch_computations={%region_4.4_spmd, %region_5.7_spmd} | conditional | flops 818681856 | bytes 36118616 | solution.py:100
  98.6 2.1 multiply_add_fusion
  102.8 8.6 %collective-permute-done = bf16[2,512,2,128]{3,1,2,0:T(8,128)(2,1)S(1)} collective-permute-done((bf16[2,512,2,128]{3,1,2,0:T(8,128)(2,1)}, bf16[2,512,2,128]{3,1,2,0:T(8,128)(2,1)S(1)}, u32[]{:S(2)}, u32[]{:S(2)}) %collective-permute-start) | collective-permute-done | bytes 524320 | tf_op jit(solution)/shard_map/while/body/eval_jaxpr/ppermute | solution.py:92
  111.4 5.7 %conditional.2 = ((f32[2,3,512]{2,1,0:T(4,128)S(1)}, f32[2,3,512]{2,1,0:T(4,128)S(1)}, f32[2,3,512,128]{3,2,1,0:T(8,128)})) conditional(s32[]{:T(128)} %convert_element_type.92, (f32[2,3,512]{2,1,0:T(4,128)S(1)}, f32[2,3,512]{2,1,0:T(4,128)S(1)}, f32[2,3,512,128]{3,2,1,0:T(8,128)}) %tuple.51, (bf16[2,512,2,128]{3,1,2,0:T(8,128)(2,1)S(1)}, ...), branch_computations={%region_4.4_spmd, %region_5.7_spmd} | conditional | flops 818681856 | bytes 36118616 | solution.py:100
  113.8 2.1 multiply_add_fusion
  117.9 8.6 %collective-permute-done = bf16[2,512,2,128]{3,1,2,0:T(8,128)(2,1)S(1)} collective-permute-done((bf16[2,512,2,128]{3,1,2,0:T(8,128)(2,1)}, bf16[2,512,2,128]{3,1,2,0:T(8,128)(2,1)S(1)}, u32[]{:S(2)}, u32[]{:S(2)}) %collective-permute-start) | collective-permute-done | bytes 524320 | tf_op jit(solution)/shard_map/while/body/eval_jaxpr/ppermute | solution.py:92
  126.5 5.7 %conditional.2 = ((f32[2,3,512]{2,1,0:T(4,128)S(1)}, f32[2,3,512]{2,1,0:T(4,128)S(1)}, f32[2,3,512,128]{3,2,1,0:T(8,128)})) conditional(s32[]{:T(128)} %convert_element_type.92, (f32[2,3,512]{2,1,0:T(4,128)S(1)}, f32[2,3,512]{2,1,0:T(4,128)S(1)}, f32[2,3,512,128]{3,2,1,0:T(8,128)}) %tuple.51, (bf16[2,512,2,128]{3,1,2,0:T(8,128)(2,1)S(1)}, ...), branch_computations={%region_4.4_spmd, %region_5.7_spmd} | conditional | flops 818681856 | bytes 36118616 | solution.py:100
  128.9 2.1 multiply_add_fusion
  133.0 8.6 %collective-permute-done = bf16[2,512,2,128]{3,1,2,0:T(8,128)(2,1)S(1)} collective-permute-done((bf16[2,512,2,128]{3,1,2,0:T(8,128)(2,1)}, bf16[2,512,2,128]{3,1,2,0:T(8,128)(2,1)S(1)}, u32[]{:S(2)}, u32[]{:S(2)}) %collective-permute-start) | collective-permute-done | bytes 524320 | tf_op jit(solution)/shard_map/while/body/eval_jaxpr/ppermute | solution.py:92
  142.4 6.2 %bitcast_convert_fusion = bf16[512,3072]{1,0:T(8,128)(2,1)} fusion(bf16[2,3,128,3072]{3,2,1,0:T(8,128)(2,1)} %bitcast.70, f32[2,3,512,128]{3,2,1,0:T(8,128)} %get-tuple-element.158, f32[2,3,512]{2,1,0:T(4,128)S(1)} %get-tuple-element.159), kind=kOutput, calls=%fused_computation.24 | convolution fusion | flops 2418278400 | bytes 9449472 | tf_op jit(solution)/shard_map/ngte,ngef->tf/dot_general | solution.py:73
  151.4 70.5 %all-reduce.2.cloned.1.call-done = bf16[512,3072]{1,0:T(8,128)(2,1)} async-done(((bf16[512,3072]{1,0:T(8,128)(2,1)}), bf16[512,3072]{1,0:T(8,128)(2,1)}) %all-reduce.2.cloned.1.call-update) | async-done | bytes 3145744 | tf_op jit(solution)/shard_map/psum | solution.py:74
  221.9 5.7 %fusion.18 = bf16[512,3072]{1,0:T(8,128)(2,1)} fusion(bf16[512,3072]{1,0:T(8,128)(2,1)} %param.11, bf16[512,3072]{1,0:T(8,128)(2,1)} %all-reduce.2.cloned.1.call-done), kind=kLoop, calls=%fused_computation.23 | loop fusion | flops 6291456 | bytes 9437184 | tf_op jit(solution)/shard_map/convert_element_type | solution.py:75
  (115 shorter events, 40.8 us)
Async XLA Ops:
  7.2 5.6 %copy-start = (bf16[3072,256]{1,0:T(8,128)(2,1)S(1)}, bf16[3072,256]{1,0:T(8,128)(2,1)}, u32[]{:S(2)}) copy-start(bf16[3072,256]{1,0:T(8,128)(2,1)} %param.15) | copy-start | bytes 4718596
  7.2 214.7 %all-reduce.2.cloned.1.call-start = ((), (), s32[]{:S(2)}) async-start(), calls=%async_computation | async-start | bytes 6291456 | tf_op jit(solution)/shard_map/psum | solution.py:74
  7.3 5.6 %copy-start.3 = (bf16[512,3072]{1,0:T(8,128)(2,1)S(1)}, bf16[512,3072]{1,0:T(8,128)(2,1)}, u32[]{:S(2)}) copy-start(bf16[512,3072]{1,0:T(8,128)(2,1)} %param.11) | copy-start | bytes 9437188
  27.6 4.7 %copy-start.11 = (f32[512,2,64]{2,0,1:T(8,128)S(1)}, f32[512,2,64]{2,0,1:T(8,128)}, u32[]{:S(2)}) copy-start(f32[512,2,64]{2,0,1:T(8,128)} %copy.45) | copy-start | bytes 786436
  27.6 4.7 %copy-start.12 = (f32[512,2,64]{2,0,1:T(8,128)S(1)}, f32[512,2,64]{2,0,1:T(8,128)}, u32[]{:S(2)}) copy-start(f32[512,2,64]{2,0,1:T(8,128)} %copy.46) | copy-start | bytes 786436
  31.3 5.5 %copy-start.13 = (bf16[512,256]{0,1:T(8,128)(2,1)}, bf16[512,256]{0,1:T(8,128)(2,1)S(1)}, u32[]{:S(2)}) copy-start(bf16[512,256]{0,1:T(8,128)(2,1)S(1)} %convolution_convert_fusion) | copy-start | bytes 786436
  31.3 2.1 copy-start.4
  32.5 0.8 copy-start.9
  33.5 0.9 copy-start.5
  36.9 4.4 %copy-start.8 = (bf16[512,2,64]{2,0,1:T(8,128)(2,1)S(1)}, bf16[512,2,64]{2,0,1:T(8,128)(2,1)}, u32[]{:S(2)}) copy-start(bf16[512,2,64]{2,0,1:T(8,128)(2,1)} %copy-done.7) | copy-start | bytes 393220
  36.9 4.4 %copy-start.10 = (bf16[512,2,64]{2,0,1:T(8,128)(2,1)S(1)}, bf16[512,2,64]{2,0,1:T(8,128)(2,1)}, u32[]{:S(2)}) copy-start(bf16[512,2,64]{2,0,1:T(8,128)(2,1)} %copy-done.9) | copy-start | bytes 393220
  42.2 8.6 %collective-permute-start = (bf16[2,512,2,128]{3,1,2,0:T(8,128)(2,1)}, bf16[2,512,2,128]{3,1,2,0:T(8,128)(2,1)S(1)}, u32[]{:S(2)}, u32[]{:S(2)}) collective-permute-start(bf16[2,512,2,128]{3,1,2,0:T(8,128)(2,1)} %get-tuple-element.260), channel_id=1, source_target_pairs={{0,1},{1,2},{2,3},{3,4},{4,5},{5,6},{6,7},{7,0},{8,9},{9,10},{10,1... | collective-permute-start | bytes 1572872 | tf_op jit(solution)/shard_map/while/body/eval_jaxpr/ppermute | solution.py:92
  51.8 1.4 copy-start.1
  55.4 1.2 copy-start.2
  57.3 8.6 %collective-permute-start = (bf16[2,512,2,128]{3,1,2,0:T(8,128)(2,1)}, bf16[2,512,2,128]{3,1,2,0:T(8,128)(2,1)S(1)}, u32[]{:S(2)}, u32[]{:S(2)}) collective-permute-start(bf16[2,512,2,128]{3,1,2,0:T(8,128)(2,1)} %get-tuple-element.260), channel_id=1, source_target_pairs={{0,1},{1,2},{2,3},{3,4},{4,5},{5,6},{6,7},{7,0},{8,9},{9,10},{10,1... | collective-permute-start | bytes 1572872 | tf_op jit(solution)/shard_map/while/body/eval_jaxpr/ppermute | solution.py:92
  67.0 1.4 copy-start.1
  70.5 1.2 copy-start.2
  72.5 8.6 %collective-permute-start = (bf16[2,512,2,128]{3,1,2,0:T(8,128)(2,1)}, bf16[2,512,2,128]{3,1,2,0:T(8,128)(2,1)S(1)}, u32[]{:S(2)}, u32[]{:S(2)}) collective-permute-start(bf16[2,512,2,128]{3,1,2,0:T(8,128)(2,1)} %get-tuple-element.260), channel_id=1, source_target_pairs={{0,1},{1,2},{2,3},{3,4},{4,5},{5,6},{6,7},{7,0},{8,9},{9,10},{10,1... | collective-permute-start | bytes 1572872 | tf_op jit(solution)/shard_map/while/body/eval_jaxpr/ppermute | solution.py:92
  82.1 1.4 copy-start.1
  85.7 1.2 copy-start.2
  87.6 8.6 %collective-permute-start = (bf16[2,512,2,128]{3,1,2,0:T(8,128)(2,1)}, bf16[2,512,2,128]{3,1,2,0:T(8,128)(2,1)S(1)}, u32[]{:S(2)}, u32[]{:S(2)}) collective-permute-start(bf16[2,512,2,128]{3,1,2,0:T(8,128)(2,1)} %get-tuple-element.260), channel_id=1, source_target_pairs={{0,1},{1,2},{2,3},{3,4},{4,5},{5,6},{6,7},{7,0},{8,9},{9,10},{10,1... | collective-permute-start | bytes 1572872 | tf_op jit(solution)/shard_map/while/body/eval_jaxpr/ppermute | solution.py:92
  97.2 1.4 copy-start.1
  100.8 1.2 copy-start.2
  102.7 8.6 %collective-permute-start = (bf16[2,512,2,128]{3,1,2,0:T(8,128)(2,1)}, bf16[2,512,2,128]{3,1,2,0:T(8,128)(2,1)S(1)}, u32[]{:S(2)}, u32[]{:S(2)}) collective-permute-start(bf16[2,512,2,128]{3,1,2,0:T(8,128)(2,1)} %get-tuple-element.260), channel_id=1, source_target_pairs={{0,1},{1,2},{2,3},{3,4},{4,5},{5,6},{6,7},{7,0},{8,9},{9,10},{10,1... | collective-permute-start | bytes 1572872 | tf_op jit(solution)/shard_map/while/body/eval_jaxpr/ppermute | solution.py:92
  112.4 1.4 copy-start.1
  115.9 1.2 copy-start.2
  117.9 8.6 %collective-permute-start = (bf16[2,512,2,128]{3,1,2,0:T(8,128)(2,1)}, bf16[2,512,2,128]{3,1,2,0:T(8,128)(2,1)S(1)}, u32[]{:S(2)}, u32[]{:S(2)}) collective-permute-start(bf16[2,512,2,128]{3,1,2,0:T(8,128)(2,1)} %get-tuple-element.260), channel_id=1, source_target_pairs={{0,1},{1,2},{2,3},{3,4},{4,5},{5,6},{6,7},{7,0},{8,9},{9,10},{10,1... | collective-permute-start | bytes 1572872 | tf_op jit(solution)/shard_map/while/body/eval_jaxpr/ppermute | solution.py:92
  127.5 1.4 copy-start.1
  131.1 1.2 copy-start.2
  133.0 8.6 %collective-permute-start = (bf16[2,512,2,128]{3,1,2,0:T(8,128)(2,1)}, bf16[2,512,2,128]{3,1,2,0:T(8,128)(2,1)S(1)}, u32[]{:S(2)}, u32[]{:S(2)}) collective-permute-start(bf16[2,512,2,128]{3,1,2,0:T(8,128)(2,1)} %get-tuple-element.260), channel_id=1, source_target_pairs={{0,1},{1,2},{2,3},{3,4},{4,5},{5,6},{6,7},{7,0},{8,9},{9,10},{10,1... | collective-permute-start | bytes 1572872 | tf_op jit(solution)/shard_map/while/body/eval_jaxpr/ppermute | solution.py:92
  148.6 0.9 copy-start.6
  148.6 1.9 copy-start.14
  (1 other events, 0.7 us)
Sparse Core Ops, SparseCore 0:
  148.8 73.0 all-reduce.1
where the time goes:
time: 236 us; the launch traced here: 234 us
  waiting for transfers between devices  131 us (56%)
  matrix products  40.1 us (17%)
  local copies, waits for them, and re-layouts  26.8 us (11%)
  other arithmetic  22.1 us (9%)
  between operations  14.3 us (6%)
    psum x1, waiting for transfers between devices, output_sum(): attn_sum = lax.psum(part_sum, 'tp')  70.5 us
    ppermute x7, waiting for transfers between devices, shift_step(): kv_blk = lax.ppermute(kv_blk, 'cp', shift_pairs)  60.2 us
    dot_general x6, matrix products, attend_block(): jnp.einsum('ohut,tof->ohuf', weights.astype(jnp.bfloat16), kv_blk[1], pre...  12.8 us
    unnamed x32, local copies, waits for them, and re-layouts  9.93 us
    cond x30, local copies, waits for them, and re-layouts  8.89 us
    reduce_sum x6, other arithmetic, attend_block(): new_sum = run_sum * rescale + jnp.sum(weights, axis=-1)  6.3 us
    dot_general x1, matrix products, output_sum(): jnp.einsum('ngte,ngef->tf', attn_o, w_out_r, preferred_element_type=jnp.f...  6.19 us
    dot_general x6, matrix products, attend_block(): jnp.einsum('uohf,tof->ohut', queries, kv_blk[0], preferred_element_type=j...  5.96 us
  transfers between devices with their start and end apart: 8, of which 8 were waited for; matrix products, arithmetic and copies ran while one was open for 1% of the time, Pallas kernels for 0%

commit v1 on v0

v1 whole, which is shorter than its diff:
```python
import math
import jax
import jax.numpy as jnp
from jax import lax
from jax.experimental import pallas as pl
from jax.experimental.pallas import tpu as pltpu
from jax.sharding import PartitionSpec as P

HEAD = 128
EPS = 1e-5
LOG_THETA = math.log(1000000.0)
SCORE_EXP2 = math.log2(math.e) / math.sqrt(HEAD)
BF = jnp.bfloat16
F32 = jnp.float32
GROUPS = 4
Q_TILE = 256
NORM_ROWS = 32


def rope_tables(positions):
    half_dim = HEAD // 2
    inv_freq = jnp.exp(jnp.arange(half_dim, dtype=F32) * (-2.0 * LOG_THETA / HEAD))
    angles = positions.astype(F32)[:, None] * inv_freq
    cos_t, sin_t = jnp.cos(angles), jnp.sin(angles)
    return jnp.concatenate([cos_t, cos_t], axis=-1), jnp.concatenate([-sin_t, sin_t], axis=-1)


def block_kernel(ring, kv_heads, group_size,
                 x_hbm, gain_ref, cos_ref, sin_ref, wq_hbm, wk_hbm, wv_hbm, wo_hbm,
                 out_hbm, k_hbm, v_hbm,
                 x_v, h_v, wq_v, wk_v, wv_v, wo_v, q_v, kv_v, m_v, l_v, acc_v, o_v,
                 part_v, r1_v, r2_v, out_v,
                 load_sem, cache_sem, kv_send, kv_recv, kv_fwd_send,
                 s1_send, s1_recv, s2_send, s2_recv, f1_send, f1_recv, f2_send, f2_recv, out_sem):
    rows, width = x_v.shape
    cp = lax.axis_index('cp')
    tp = lax.axis_index('tp')
    chip = cp // 2
    core = cp % 2
    seg_rows = rows // ring
    half_cols = width // (2 * GROUPS)

    x_right = {'cp': ((chip + 1) % ring) * 2 + core}
    x_left = {'cp': ((chip + ring - 1) % ring) * 2 + core}
    sibling = {'cp': chip * 2 + 1 - core}
    y_right = {'tp': (tp + 1) % ring}
    y_left = {'tp': (tp + ring - 1) % ring}

    loads = [
        pltpu.make_async_copy(x_hbm, x_v, load_sem.at[0]),
        pltpu.make_async_copy(wk_hbm, wk_v, load_sem.at[1]),
        pltpu.make_async_copy(wv_hbm, wv_v, load_sem.at[2]),
        pltpu.make_async_copy(wq_hbm, wq_v, load_sem.at[3]),
        pltpu.make_async_copy(wo_hbm, wo_v, load_sem.at[4]),
    ]
    for copy in loads:
        copy.start()

    barrier = pltpu.get_barrier_semaphore()
    for peer in (x_right, x_left, sibling, y_right, y_left):
        pl.semaphore_signal(barrier, inc=1, device_id=peer, device_id_type=pl.DeviceIdType.MESH)

    loads[0].wait()

    def norm_step(i, carry):
        r0 = pl.multiple_of(i * NORM_ROWS, NORM_ROWS)
        xf = x_v[pl.ds(r0, NORM_ROWS), :].astype(F32)
        inv = lax.rsqrt(jnp.mean(xf * xf, axis=-1, keepdims=True) + EPS)
        h_v[pl.ds(r0, NORM_ROWS), :] = (xf * inv * gain_ref[...].astype(F32)).astype(BF)
        return carry

    lax.fori_loop(0, rows // NORM_ROWS, norm_step, 0)

    def rope(vals):
        return (vals * cos_ref[...] + pltpu.roll(vals, HEAD // 2, 1) * sin_ref[...]).astype(BF)

    loads[1].wait()
    k_proj = jnp.dot(h_v[...], wk_v[...], preferred_element_type=F32)
    for h in range(kv_heads):
        kv_v[0, 0, h, 0] = rope(k_proj[:, h * HEAD:(h + 1) * HEAD])
    loads[2].wait()
    v_proj = jnp.dot(h_v[...], wv_v[...], preferred_element_type=F32)
    for h in range(kv_heads):
        kv_v[0, 0, h, 1] = v_proj[:, h * HEAD:(h + 1) * HEAD].astype(BF)

    pl.semaphore_wait(barrier, 5)

    def remote(src, dst, send, recv, peer):
        return pltpu.make_async_remote_copy(src_ref=src, dst_ref=dst, send_sem=send, recv_sem=recv,
                                            device_id=peer, device_id_type=pl.DeviceIdType.MESH)

    def own_to(rel, cc, head, peer):
        return remote(kv_v.at[0, 0, head], kv_v.at[rel, cc, head],
                      kv_send.at[rel, head], kv_recv.at[rel, cc, head], peer)

    def fwd_far(head):
        rel, peer = (1, x_right) if head == 1 else (2, x_left)
        return remote(kv_v.at[rel, 0, head], kv_v.at[3, 0, head],
                      kv_send.at[3, head], kv_recv.at[3, 0, head], peer)

    def fwd_sib(rel, head):
        return remote(kv_v.at[rel, 0, head], kv_v.at[rel, 1, head],
                      kv_fwd_send.at[rel, head], kv_recv.at[rel, 1, head], sibling)

    right_sends = chip < ring - 1
    left_h0_sends = chip < 2
    left_h1_sends = chip < 1

    @pl.when(core == 0)
    def _():
        own_to(0, 1, 0, sibling).start()
        own_to(0, 1, 1, sibling).start()

    @pl.when(right_sends)
    def _():
        own_to(1, 0, 1, x_right).start()

    @pl.when(left_h0_sends)
    def _():
        own_to(2, 0, 0, x_left).start()

    @pl.when(right_sends)
    def _():
        own_to(1, 0, 0, x_right).start()

    @pl.when(left_h1_sends)
    def _():
        own_to(2, 0, 1, x_left).start()

    cache_copies = []
    for h in range(kv_heads):
        for kv, dst in ((0, k_hbm), (1, v_hbm)):
            cache_copies.append(pltpu.make_async_copy(
                kv_v.at[0, 0, h, kv], dst.at[:, h * HEAD:(h + 1) * HEAD], cache_sem.at[h, kv]))
    for copy in cache_copies:
        copy.start()

    loads[3].wait()

    def q_step(j, carry):
        c0 = pl.multiple_of(j * 2 * HEAD, 2 * HEAD)
        q_proj = jnp.dot(h_v[...], wq_v[:, pl.ds(c0, 2 * HEAD)], preferred_element_type=F32)
        q_v[2 * j] = rope(q_proj[:, :HEAD])
        q_v[2 * j + 1] = rope(q_proj[:, HEAD:])
        return carry

    lax.fori_loop(0, kv_heads * group_size // 2, q_step, 0)

    def scores(q_tile, k_tile):
        return lax.dot_general(q_tile, k_tile, (((1,), (1,)), ((), ())), preferred_element_type=F32)

    def lane_chunks(s):
        return [s[:, i * HEAD:(i + 1) * HEAD] for i in range(s.shape[1] // HEAD)]

    def tree(op, parts):
        parts = list(parts)
        while len(parts) > 1:
            parts = [op(parts[i], parts[i + 1]) if i + 1 < len(parts) else parts[i] for i in range(0, len(parts), 2)]
        return parts[0]

    def row_max(chunks):
        return jnp.max(tree(jnp.maximum, chunks), axis=1, keepdims=True)

    def weights(chunks, m_new):
        probs = [jnp.exp2((s - m_new) * SCORE_EXP2) for s in chunks]
        return probs, tree(jnp.add, probs)

    def pv(probs, v_tile):
        return jnp.dot(jnp.concatenate([p.astype(BF) for p in probs], axis=1), v_tile, preferred_element_type=F32)

    def own_unit(qi, carry):
        head = qi // group_size
        for rt in range(rows // Q_TILE):
            r0, keys = rt * Q_TILE, (rt + 1) * Q_TILE
            s = scores(q_v[qi, r0:r0 + Q_TILE, :], kv_v[0, 0, head, 0, :keys, :])
            row_id = lax.broadcasted_iota(jnp.int32, s.shape, 0) + r0
            col_id = lax.broadcasted_iota(jnp.int32, s.shape, 1)
            chunks = lane_chunks(jnp.where(col_id <= row_id, s, -jnp.inf))
            m_new = jnp.broadcast_to(row_max(chunks), (Q_TILE, HEAD))
            probs, l_new = weights(chunks, m_new)
            acc_v[qi, r0:r0 + Q_TILE, :] = pv(probs, kv_v[0, 0, head, 1, :keys, :])
            m_v[qi, r0:r0 + Q_TILE, :] = m_new
            l_v[qi, r0:r0 + Q_TILE, :] = l_new
        return carry

    lax.fori_loop(0, kv_heads * group_size, own_unit, 0)

    def far_unit(rel, cc, head):
        def q_head(g, carry):
            qi = head * group_size + g
            for rt in range(rows // Q_TILE):
                rs = slice(rt * Q_TILE, (rt + 1) * Q_TILE)
                chunks = lane_chunks(scores(q_v[qi, rs, :], kv_v[rel, cc, head, 0]))
                m_old = m_v[qi, rs, :]
                m_new = jnp.maximum(m_old, row_max(chunks))
                alpha = jnp.exp2((m_old - m_new) * SCORE_EXP2)
                probs, l_new = weights(chunks, m_new)
                acc_v[qi, rs, :] = acc_v[qi, rs, :] * alpha + pv(probs, kv_v[rel, cc, head, 1])
                l_v[qi, rs, :] = l_v[qi, rs, :] * alpha + l_new
                m_v[qi, rs, :] = m_new
            return carry

        lax.fori_loop(0, group_size, q_head, 0)

    has_left = chip >= 1
    has_right = chip >= 3
    has_far = chip >= 2
    fwd_right = jnp.logical_and(chip >= 1, chip <= 2)
    fwd_left = jnp.logical_or(chip == 0, chip == 3)

    def phase(p, carry):
        @pl.when(jnp.logical_and(p == 0, core == 1))
        def _():
            own_to(0, 1, 0, sibling).wait_recv()
            own_to(0, 1, 1, sibling).wait_recv()

        @pl.when(jnp.logical_and(p == 1, has_left))
        def _():
            own_to(1, 0, 1, x_right).wait_recv()

            @pl.when(fwd_right)
            def _():
                fwd_far(1).start()

            fwd_sib(1, 1).start()

        @pl.when(jnp.logical_and(p == 1, fwd_left))
        def _():
            own_to(2, 0, 0, x_left).wait_recv()
            fwd_far(0).start()

            @pl.when(has_right)
            def _():
                fwd_sib(2, 0).start()

        @pl.when(jnp.logical_and(p == 2, has_left))
        def _():
            own_to(1, 0, 0, x_right).wait_recv()
            fwd_sib(1, 0).start()

        @pl.when(jnp.logical_and(p == 2, has_right))
        def _():
            own_to(2, 0, 1, x_left).wait_recv()
            fwd_sib(2, 1).start()

        @pl.when(jnp.logical_and(p == 3, has_far))
        def _():
            fwd_far(1).wait_recv()
            fwd_sib(3, 1).start()
            fwd_far(0).wait_recv()
            fwd_sib(3, 0).start()

        def unit(i, inner):
            cc, which = i // 2, i % 2
            head = (p + which) % 2
            rel = ((p + 2) // 3) * (1 + which) + (p // 3) * (2 - which)
            need = ((p == 0) & (cc == 1) & (core == 1)) | ((rel == 1) & has_left) | ((rel == 2) & has_right) | ((rel == 3) & has_far)

            @pl.when(need & (p > 0) & (cc == 1))
            def _():
                remote(kv_v.at[rel, 0, head], kv_v.at[rel, 1, head], kv_fwd_send.at[rel, head],
                       kv_recv.at[rel, 1, head], sibling).wait_recv()

            @pl.when(need)
            def _():
                far_unit(rel, cc, head)

            return inner

        lax.fori_loop(0, 4, unit, 0)
        return carry

    lax.fori_loop(0, 4, phase, 0)

    def norm_out(qi, carry):
        l_row = jnp.sum(l_v[qi], axis=1, keepdims=True)
        c0 = pl.multiple_of(qi * HEAD, HEAD)
        o_v[:, pl.ds(c0, HEAD)] = (acc_v[qi] / l_row).astype(BF)
        return carry

    lax.fori_loop(0, kv_heads * group_size, norm_out, 0)
    loads[4].wait()

    def seg(offset):
        return pl.ds(pl.multiple_of(((tp + offset + ring) % ring) * seg_rows, seg_rows), seg_rows)

    def s1(g, d):
        return remote(part_v.at[g, d, seg(2), :], r1_v.at[g, d], s1_send.at[g, d], s1_recv.at[g, d],
                      y_left if d else y_right)

    def s2(g, d, half):
        return remote(part_v.at[g, half, seg(-1 if d else 1), :], r2_v.at[g, d, half],
                      s2_send.at[g, d, half], s2_recv.at[g, d, half], y_left if d else y_right)

    def f1(g, d):
        return remote(out_v.at[g, :, seg(0), :], out_v.at[g, :, seg(0), :], f1_send.at[g, d], f1_recv.at[g, d],
                      y_left if d else y_right)

    def f1_arrival(g, d):
        own = seg(1 if d else -1)
        return remote(out_v.at[g, :, own, :], out_v.at[g, :, own, :], f1_send.at[g, d], f1_recv.at[g, d],
                      y_left if d else y_right)

    def f2(g, d):
        own = seg(1 if d else -1)
        return remote(out_v.at[g, d, own, :], out_v.at[g, d, own, :], f2_send.at[g, d], f2_recv.at[g, d],
                      y_left if d else y_right)

    def f2_arrival(g, d):
        return remote(out_v.at[g, d, seg(2), :], out_v.at[g, d, seg(2), :], f2_send.at[g, d], f2_recv.at[g, d],
                      y_left if d else y_right)

    def write(g, offset, half, slot):
        c0 = pl.multiple_of((2 * g + half) * half_cols, half_cols)
        return pltpu.make_async_copy(out_v.at[g, half, seg(offset), :], out_hbm.at[seg(offset), pl.ds(c0, half_cols)],
                                     out_sem.at[g, slot, half])

    def project(g, carry):
        for half in range(2):
            c0 = pl.multiple_of((2 * g + half) * half_cols, half_cols)
            part_v[g, half] = jnp.dot(o_v[...], wo_v[:, pl.ds(c0, half_cols)], preferred_element_type=F32).astype(BF)
        for d in range(2):
            s1(g, d).start()
        for d in range(2):
            s2(g, d, 1 - d).start()
        return carry

    lax.fori_loop(0, GROUPS, project, 0)

    def add_first(g, carry):
        for d in range(2):
            s1(g, d).wait_recv()
            rs = seg(-1 if d else 1)
            part_v[g, d, rs, :] = (part_v[g, d, rs, :].astype(F32) + r1_v[g, d].astype(F32)).astype(BF)
            s2(g, d, d).start()
        return carry

    lax.fori_loop(0, GROUPS, add_first, 0)

    def add_last(g, carry):
        for d in range(2):
            for half in range(2):
                s2(g, d, half).wait_recv()
        for half in range(2):
            c0 = pl.multiple_of((2 * g + half) * half_cols, half_cols)
            attn = part_v[g, half, seg(0), :].astype(F32) + r2_v[g, 0, half].astype(F32) + r2_v[g, 1, half].astype(F32)
            out_v[g, half, seg(0), :] = (x_v[seg(0), pl.ds(c0, half_cols)].astype(F32) + attn).astype(BF)
        for d in range(2):
            f1(g, d).start()
        for half in range(2):
            write(g, 0, half, 0).start()
        return carry

    lax.fori_loop(0, GROUPS, add_last, 0)

    def pass_on(g, carry):
        for d in range(2):
            f1_arrival(g, d).wait_recv()
            f2(g, d).start()
            for half in range(2):
                write(g, 1 if d else -1, half, 1 + d).start()
        return carry

    lax.fori_loop(0, GROUPS, pass_on, 0)

    def finish(g, carry):
        for d in range(2):
            f2_arrival(g, d).wait_recv()
            write(g, 2, d, 3).start()
        return carry

    lax.fori_loop(0, GROUPS, finish, 0)

    def drain(g, carry):
        for d in range(2):
            s1(g, d).wait_send()
            for half in range(2):
                s2(g, d, half).wait_send()
            f1(g, d).wait_send()
            f2(g, d).wait_send()
        for half in range(2):
            for slot, offset in enumerate((0, -1, 1, 2)):
                write(g, offset, half, slot).wait()
        return carry

    lax.fori_loop(0, GROUPS, drain, 0)

    for copy in cache_copies:
        copy.wait()

    @pl.when(core == 0)
    def _():
        own_to(0, 1, 0, sibling).wait_send()
        own_to(0, 1, 1, sibling).wait_send()

    @pl.when(right_sends)
    def _():
        own_to(1, 0, 1, x_right).wait_send()
        own_to(1, 0, 0, x_right).wait_send()

    @pl.when(left_h0_sends)
    def _():
        own_to(2, 0, 0, x_left).wait_send()

    @pl.when(left_h1_sends)
    def _():
        own_to(2, 0, 1, x_left).wait_send()

    @pl.when(has_left)
    def _():
        fwd_sib(1, 0).wait_send()
        fwd_sib(1, 1).wait_send()

    @pl.when(has_right)
    def _():
        fwd_sib(2, 0).wait_send()
        fwd_sib(2, 1).wait_send()

    @pl.when(has_far)
    def _():
        fwd_sib(3, 0).wait_send()
        fwd_sib(3, 1).wait_send()

    @pl.when(fwd_right)
    def _():
        fwd_far(1).wait_send()

    @pl.when(fwd_left)
    def _():
        fwd_far(0).wait_send()


def solution(mesh):
    ring = mesh.shape['tp']
    if mesh.shape['cp'] != 2 * ring or ring != 4:
        raise ValueError('mesh')
    row_spec = P(('dp', 'cp'), None)
    cache_spec = P(('dp', 'cp'), 'tp', None)
    head_cols = P(None, 'tp')

    def local_block(hidden, positions, norm_gain, w_query, w_key, w_value, w_out):
        rows, width = hidden.shape
        kv_heads = w_key.shape[1] // HEAD
        q_heads = w_query.shape[1] // HEAD
        seg_rows, half_cols = rows // ring, width // (2 * GROUPS)
        cos_t, sin_t = rope_tables(positions)
        dma = pltpu.SemaphoreType.DMA
        out, k_new, v_new = pl.pallas_call(
            lambda *refs: block_kernel(ring, kv_heads, q_heads // kv_heads, *refs),
            out_shape=(
                jax.ShapeDtypeStruct((rows, width), BF),
                jax.ShapeDtypeStruct((rows, kv_heads * HEAD), BF),
                jax.ShapeDtypeStruct((rows, kv_heads * HEAD), BF),
            ),
            in_specs=[pl.BlockSpec(memory_space=pl.ANY)] + [pl.BlockSpec(memory_space=pltpu.VMEM)] * 3
            + [pl.BlockSpec(memory_space=pl.ANY)] * 4,
            out_specs=[pl.BlockSpec(memory_space=pl.ANY)] * 3,
            scratch_shapes=[
                pltpu.VMEM((rows, width), BF),
                pltpu.VMEM((rows, width), BF),
                pltpu.VMEM(w_query.shape, BF),
                pltpu.VMEM(w_key.shape, BF),
                pltpu.VMEM(w_value.shape, BF),
                pltpu.VMEM(w_out.shape, BF),
                pltpu.VMEM((q_heads, rows, HEAD), BF),
                pltpu.VMEM((4, 2, kv_heads, 2, rows, HEAD), BF),
                pltpu.VMEM((q_heads, rows, HEAD), F32),
                pltpu.VMEM((q_heads, rows, HEAD), F32),
                pltpu.VMEM((q_heads, rows, HEAD), F32),
                pltpu.VMEM((rows, q_heads * HEAD), BF),
                pltpu.VMEM((GROUPS, 2, rows, half_cols), BF),
                pltpu.VMEM((GROUPS, 2, seg_rows, half_cols), BF),
                pltpu.VMEM((GROUPS, 2, 2, seg_rows, half_cols), BF),
                pltpu.VMEM((GROUPS, 2, rows, half_cols), BF),
                dma((5,)),
                dma((kv_heads, 2)),
                dma((4, kv_heads)),
                dma((4, 2, kv_heads)),
                dma((4, kv_heads)),
                dma((GROUPS, 2)), dma((GROUPS, 2)),
                dma((GROUPS, 2, 2)), dma((GROUPS, 2, 2)),
                dma((GROUPS, 2)), dma((GROUPS, 2)),
                dma((GROUPS, 2)), dma((GROUPS, 2)),
                dma((GROUPS, 4, 2)),
            ],
            compiler_params=pltpu.CompilerParams(collective_id=0, has_side_effects=True, vmem_limit_bytes=60 * 1024 * 1024),
            name='attn_block',
        )(hidden, norm_gain.reshape(1, width), cos_t, sin_t, w_query, w_key, w_value, w_out)
        cache_shape = (rows, kv_heads, HEAD)
        return out, k_new.reshape(cache_shape), v_new.reshape(cache_shape)

    return jax.shard_map(local_block, mesh=mesh,
                         in_specs=(row_spec, P(('dp', 'cp')), P(None), head_cols, head_cols, head_cols, P('tp', None)),
                         out_specs=(row_spec, cache_spec, cache_spec), check_vma=False)
```

time: 236 us -> 120 us (0.51)
  the two profiles are of different devices: /device:TPU:102 before, /device:TPU:103 now
where the time goes in v1:
time: 120 us; the launch traced here: 119 us
  Pallas kernels  107 us (89%)
  local copies, waits for them, and re-layouts  8.49 us (7%)
  other arithmetic  2.68 us (2%)
    pallas_call x1, Pallas kernels, local_block(): pl.pallas_call(lambda *refs: block_kernel(ring, kv_heads, q_heads // kv_h...  107 us
    unnamed x1, local copies, waits for them, and re-layouts  3.76 us
    reshape x2, local copies, waits for them, and re-layouts, local_block(): return (out, k_new.reshape(cache_shape), v_new.reshape(cache_shape))  3.43 us

profile of v1, /device:TPU:103, one launch (start us, length us, event | category | flops | bytes accessed | tf_op | source)
XLA Modules:
  0.0 119.3 jit_solution(2447077900162486814)
XLA Ops:
  0.6 0.7 convert_element_type.3
  1.3 1.3 %reshape.21.refs_1_ = bf16[1,3072]{1,0:T(2,128)(2,1)} reshape(bf16[3072]{0:T(1024)(128)(2,1)} %param.9) | data formatting | bytes 12288 | tf_op jit(solution)/shard_map/reshape | solution.py:488
  2.6 1.0 fusion
  3.6 1.0 pad_maximum_fusion
  4.6 107.5 %attn_block.1 = (bf16[512,3072]{1,0:T(8,128)(2,1)}, bf16[512,256]{1,0:T(8,128)(2,1)}, bf16[512,256]{1,0:T(8,128)(2,1)}) custom-call(bf16[512,3072]{1,0:T(8,128)(2,1)} %refs_0_.1, bf16[1,3072]{1,0:T(2,128)(2,1)} %reshape.21.refs_1_, f32[512,128]{1,0:T(8,128)} %get-tuple-element.12.refs_2_, f32[512,128]{1,0:T(8,128)} %get-tuple-element.13.refs_3_, ...), custom_call_target="tpu_custom_call" | custom-call | tf_op jit(solution)/shard_map/attn_block/pallas_call | solution.py:448
  112.1 1.7 %reshape.22 = bf16[512,2,128]{2,1,0:T(2,128)(2,1)} reshape(bf16[512,256]{1,0:T(8,128)(2,1)} %get-tuple-element.7) | data formatting | bytes 524288 | tf_op jit(solution)/shard_map/reshape | solution.py:490
  113.8 1.7 %reshape.23 = bf16[512,2,128]{2,1,0:T(2,128)(2,1)} reshape(bf16[512,256]{1,0:T(8,128)(2,1)} %get-tuple-element.8) | data formatting | bytes 524288 | tf_op jit(solution)/shard_map/reshape | solution.py:490
  115.6 3.8 %copy.11 = bf16[512,3072]{1,0:T(8,128)(2,1)} copy(bf16[512,3072]{1,0:T(8,128)(2,1)} %get-tuple-element.17) | data formatting | bytes 6291456
  (1 shorter events, 0.0 us)

commit v2 on v1

v2 whole, which is shorter than its diff:
```python
import math
import jax
import jax.numpy as jnp
import numpy as np
from jax import lax
from jax.experimental import pallas as pl
from jax.experimental.pallas import tpu as pltpu
from jax.sharding import PartitionSpec as P

HEAD = 128
EPS = 1e-5
LOG_THETA = math.log(1000000.0)
SCORE_EXP2 = math.log2(math.e) / math.sqrt(HEAD)
BF = jnp.bfloat16
F32 = jnp.float32
GROUPS = 6
Q_TILE = 256
NORM_ROWS = 32
LOAD_CHUNKS = 4


def inverse_freq():
    half = np.exp(np.arange(HEAD // 2, dtype=np.float64) * (-2.0 * LOG_THETA / HEAD)).astype(np.float32)
    return np.concatenate([half, half])[None, :]


def block_kernel(ring, kv_heads, group_size,
                 x_hbm, pos_ref, gain_ref, freq_ref, wq_hbm, wk_hbm, wv_hbm, wo_hbm,
                 out_v, k_out, v_out,
                 x_v, h_v, wq_v, wkv_v, wo_v, cos_v, sin_v, kc_v, vc_v, q_v, kv_v, m_v, l_v, acc_v, o_v,
                 part_v, r1_v, r2_v,
                 load_sem, kv_send, kv_recv, kv_fwd_send,
                 s1_send, s1_recv, s2_send, s2_recv, f1_send, f1_recv, f2_send, f2_recv):
    rows, width = x_v.shape
    cp = lax.axis_index('cp')
    tp = lax.axis_index('tp')
    chip = cp // 2
    core = cp % 2
    seg_rows = rows // ring
    half_cols = width // (2 * GROUPS)

    x_right = {'cp': ((chip + 1) % ring) * 2 + core}
    x_left = {'cp': ((chip + ring - 1) % ring) * 2 + core}
    sibling = {'cp': chip * 2 + 1 - core}
    y_right = {'tp': (tp + 1) % ring}
    y_left = {'tp': (tp + ring - 1) % ring}

    kv_cols = kv_heads * HEAD
    chunk = rows // LOAD_CHUNKS
    x_loads = [pltpu.make_async_copy(x_hbm.at[i * chunk:(i + 1) * chunk, :], x_v.at[i * chunk:(i + 1) * chunk, :],
                                     load_sem.at[4 + i]) for i in range(LOAD_CHUNKS)]
    loads = [
        pltpu.make_async_copy(wk_hbm, wkv_v.at[:, :kv_cols], load_sem.at[0]),
        pltpu.make_async_copy(wv_hbm, wkv_v.at[:, kv_cols:], load_sem.at[1]),
        pltpu.make_async_copy(wq_hbm, wq_v, load_sem.at[2]),
        pltpu.make_async_copy(wo_hbm, wo_v, load_sem.at[3]),
    ]
    for copy in x_loads + loads[:2]:
        copy.start()

    barrier = pltpu.get_barrier_semaphore()
    for peer in (x_right, x_left, sibling, y_right, y_left):
        pl.semaphore_signal(barrier, inc=1, device_id=peer, device_id_type=pl.DeviceIdType.MESH)

    with jax.named_scope('load_wait'):
        pos = pos_ref[...].astype(F32).reshape(rows // HEAD, HEAD)
        pos = jnp.concatenate([pos, jnp.zeros((8 - rows // HEAD, HEAD), F32)], axis=0).T
        sign = jnp.where(lax.broadcasted_iota(jnp.int32, (1, HEAD), 1) < HEAD // 2, -1.0, 1.0)
        for i in range(rows // HEAD):
            angles = pos[:, i:i + 1] * freq_ref[...]
            cos_v[i * HEAD:(i + 1) * HEAD, :] = jnp.cos(angles)
            sin_v[i * HEAD:(i + 1) * HEAD, :] = jnp.sin(angles) * sign

    def norm_step(i, carry):
        r0 = pl.multiple_of(i * NORM_ROWS, NORM_ROWS)
        xf = x_v[pl.ds(r0, NORM_ROWS), :].astype(F32)
        inv = lax.rsqrt(jnp.mean(xf * xf, axis=-1, keepdims=True) + EPS)
        h_v[pl.ds(r0, NORM_ROWS), :] = (xf * inv * gain_ref[...].astype(F32).reshape(1, width)).astype(BF)
        return carry

    with jax.named_scope('norm'):
        for i in range(LOAD_CHUNKS):
            x_loads[i].wait()
            lax.fori_loop(i * chunk // NORM_ROWS, (i + 1) * chunk // NORM_ROWS, norm_step, 0)
    for copy in loads[2:]:
        copy.start()

    def rope(vals):
        return (vals * cos_v[...] + pltpu.roll(vals, HEAD // 2, 1) * sin_v[...]).astype(BF)

    for copy in loads[:2]:
        copy.wait()
    kv_scope = jax.named_scope('kv_proj')
    kv_scope.__enter__()
    kv_proj = jnp.dot(h_v[...], wkv_v[...], preferred_element_type=F32)
    for h in range(kv_heads):
        cols = slice(h * HEAD, (h + 1) * HEAD)
        k_head = rope(kv_proj[:, cols])
        kv_v[0, 0, h, 0] = k_head
        kc_v[:, cols] = k_head
        v_head = kv_proj[:, kv_cols + h * HEAD:kv_cols + (h + 1) * HEAD].astype(BF)
        vc_v[:, cols] = v_head
        for j in range(rows // HEAD):
            kv_v[0, 0, h, 1, j * HEAD:(j + 1) * HEAD, :] = v_head[j * HEAD:(j + 1) * HEAD, :].T
    kv_scope.__exit__(None, None, None)
    with jax.named_scope('barrier'):
        pl.semaphore_wait(barrier, 5)

    def remote(src, dst, send, recv, peer):
        return pltpu.make_async_remote_copy(src_ref=src, dst_ref=dst, send_sem=send, recv_sem=recv,
                                            device_id=peer, device_id_type=pl.DeviceIdType.MESH)

    def own_to(rel, cc, head, peer):
        return remote(kv_v.at[0, 0, head], kv_v.at[rel, cc, head],
                      kv_send.at[rel, head], kv_recv.at[rel, cc, head], peer)

    def fwd_far(head):
        rel, peer = (1, x_right) if head == 1 else (2, x_left)
        return remote(kv_v.at[rel, 0, head], kv_v.at[3, 0, head],
                      kv_send.at[3, head], kv_recv.at[3, 0, head], peer)

    def fwd_sib(rel, head):
        return remote(kv_v.at[rel, 0, head], kv_v.at[rel, 1, head],
                      kv_fwd_send.at[rel, head], kv_recv.at[rel, 1, head], sibling)

    right_sends = chip < ring - 1
    left_h0_sends = chip < 2
    left_h1_sends = chip < 1

    @pl.when(core == 0)
    def _():
        own_to(0, 1, 0, sibling).start()
        own_to(0, 1, 1, sibling).start()

    @pl.when(right_sends)
    def _():
        own_to(1, 0, 1, x_right).start()

    @pl.when(left_h0_sends)
    def _():
        own_to(2, 0, 0, x_left).start()

    @pl.when(right_sends)
    def _():
        own_to(1, 0, 0, x_right).start()

    @pl.when(left_h1_sends)
    def _():
        own_to(2, 0, 1, x_left).start()

    loads[2].wait()

    def q_step(j, carry):
        c0 = pl.multiple_of(j * 2 * HEAD, 2 * HEAD)
        q_proj = jnp.dot(h_v[...], wq_v[:, pl.ds(c0, 2 * HEAD)], preferred_element_type=F32)
        q_v[2 * j] = rope(q_proj[:, :HEAD]).T
        q_v[2 * j + 1] = rope(q_proj[:, HEAD:]).T
        return carry

    with jax.named_scope('q_proj'):
        lax.fori_loop(0, kv_heads * group_size // 2, q_step, 0)

    def scores(rel, cc, head, qi, r0, keys):
        return jnp.dot(kv_v[rel, cc, head, 0, :keys, :], q_v[qi, :, r0:r0 + Q_TILE], preferred_element_type=F32)

    def attend(tiles, first):
        def start(tile):
            rel, cc, head, qi, r0 = tile
            s = scores(rel, cc, head, qi, r0, r0 + Q_TILE if first else rows)
            if first:
                key_id = lax.broadcasted_iota(jnp.int32, s.shape, 0)
                row_id = lax.broadcasted_iota(jnp.int32, s.shape, 1) + r0
                s = jnp.where(key_id <= row_id, s, -jnp.inf)
            return s

        def soften(tile, s):
            rel, cc, head, qi, r0 = tile
            rs = slice(r0, r0 + Q_TILE)
            m_new = jnp.max(s, axis=0, keepdims=True)
            alpha = None
            if not first:
                m_old = m_v[qi, :, rs]
                m_new = jnp.maximum(m_old, m_new)
                alpha = jnp.exp2((m_old - m_new) * SCORE_EXP2)
            p = jnp.exp2((s - m_new) * SCORE_EXP2)
            l_new = jnp.sum(p, axis=0, keepdims=True)
            l_v[qi, :, rs] = l_new if first else l_v[qi, :, rs] * alpha + l_new
            m_v[qi, :, rs] = m_new
            return p.astype(BF), alpha

        def gather(tile, p, alpha):
            rel, cc, head, qi, r0 = tile
            rs = slice(r0, r0 + Q_TILE)
            v_t = jnp.concatenate([kv_v[rel, cc, head, 1, j * HEAD:(j + 1) * HEAD, :] for j in range(p.shape[0] // HEAD)], axis=1)
            o_new = jnp.dot(v_t, p, preferred_element_type=F32)
            acc_v[qi, :, rs] = o_new if first else acc_v[qi, :, rs] * alpha + o_new

        s = start(tiles[0])
        held = None
        for i in range(len(tiles) + 1):
            s_next = start(tiles[i + 1]) if i + 1 < len(tiles) else None
            if held is not None:
                gather(tiles[i - 1], *held)
            if i < len(tiles):
                held = soften(tiles[i], s)
            s = s_next

    def head_tiles(rel, cc, head):
        return [(rel, cc, head, head * group_size + g, rt * Q_TILE) for g in range(group_size) for rt in range(rows // Q_TILE)]

    def own_unit(head, carry):
        attend(head_tiles(0, 0, head), True)
        return carry

    with jax.named_scope('own'):
        lax.fori_loop(0, kv_heads, own_unit, 0)

    def far_unit(rel, cc, head):
        with jax.named_scope('far'):
            attend(head_tiles(rel, cc, head), False)

    has_left = chip >= 1
    has_right = chip >= 3
    has_far = chip >= 2
    fwd_right = jnp.logical_and(chip >= 1, chip <= 2)
    fwd_left = jnp.logical_or(chip == 0, chip == 3)

    def phase(p, carry):
        @pl.when(jnp.logical_and(p == 0, core == 1))
        def _():
            own_to(0, 1, 0, sibling).wait_recv()
            own_to(0, 1, 1, sibling).wait_recv()

        @pl.when(jnp.logical_and(p == 1, has_left))
        def _():
            own_to(1, 0, 1, x_right).wait_recv()

            @pl.when(fwd_right)
            def _():
                fwd_far(1).start()

            fwd_sib(1, 1).start()

        @pl.when(jnp.logical_and(p == 1, fwd_left))
        def _():
            own_to(2, 0, 0, x_left).wait_recv()
            fwd_far(0).start()

            @pl.when(has_right)
            def _():
                fwd_sib(2, 0).start()

        @pl.when(jnp.logical_and(p == 2, has_left))
        def _():
            own_to(1, 0, 0, x_right).wait_recv()
            fwd_sib(1, 0).start()

        @pl.when(jnp.logical_and(p == 2, has_right))
        def _():
            own_to(2, 0, 1, x_left).wait_recv()
            fwd_sib(2, 1).start()

        @pl.when(jnp.logical_and(p == 3, has_far))
        def _():
            fwd_far(1).wait_recv()
            fwd_sib(3, 1).start()
            fwd_far(0).wait_recv()
            fwd_sib(3, 0).start()

        def unit(i, inner):
            cc, which = i // 2, i % 2
            head = (p + which) % 2
            rel = ((p + 2) // 3) * (1 + which) + (p // 3) * (2 - which)
            need = ((p == 0) & (cc == 1) & (core == 1)) | ((rel == 1) & has_left) | ((rel == 2) & has_right) | ((rel == 3) & has_far)

            @pl.when(need & (p > 0) & (cc == 1))
            def _():
                remote(kv_v.at[rel, 0, head], kv_v.at[rel, 1, head], kv_fwd_send.at[rel, head],
                       kv_recv.at[rel, 1, head], sibling).wait_recv()

            @pl.when(need)
            def _():
                far_unit(rel, cc, head)

            return inner

        lax.fori_loop(0, 4, unit, 0)
        return carry

    with jax.named_scope('phase'):
        lax.fori_loop(0, 4, phase, 0)

    def norm_out(qi, carry):
        c0 = pl.multiple_of(qi * HEAD, HEAD)
        o_v[:, pl.ds(c0, HEAD)] = (acc_v[qi] * (1.0 / l_v[qi])).astype(BF).T
        return carry

    with jax.named_scope('norm_out'):
        lax.fori_loop(0, kv_heads * group_size, norm_out, 0)
    loads[3].wait()

    def seg(offset):
        return pl.ds(pl.multiple_of(((tp + offset + ring) % ring) * seg_rows, seg_rows), seg_rows)

    def s1(g, d):
        return remote(part_v.at[g, d, seg(2), :], r1_v.at[g, d], s1_send.at[g, d], s1_recv.at[g, d],
                      y_left if d else y_right)

    def s2(g, d, half):
        return remote(part_v.at[g, half, seg(-1 if d else 1), :], r2_v.at[g, d, half],
                      s2_send.at[g, d, half], s2_recv.at[g, d, half], y_left if d else y_right)

    def out_at(g, offset, half=None):
        c0, cols = (2 * g * half_cols, 2 * half_cols) if half is None else ((2 * g + half) * half_cols, half_cols)
        return out_v.at[seg(offset), pl.ds(pl.multiple_of(c0, half_cols), cols)]

    def f1(g, d, offset=0):
        return remote(out_at(g, offset), out_at(g, offset), f1_send.at[g, d], f1_recv.at[g, d],
                      y_left if d else y_right)

    def f2(g, d, offset):
        return remote(out_at(g, offset, d), out_at(g, offset, d), f2_send.at[g, d], f2_recv.at[g, d],
                      y_left if d else y_right)

    def project(g, carry):
        for half in range(2):
            c0 = pl.multiple_of((2 * g + half) * half_cols, half_cols)
            part_v[g, half] = jnp.dot(o_v[...], wo_v[:, pl.ds(c0, half_cols)], preferred_element_type=F32).astype(BF)
        for d in range(2):
            s1(g, d).start()
        for d in range(2):
            s2(g, d, 1 - d).start()
        return carry

    with jax.named_scope('project'):
        lax.fori_loop(0, GROUPS, project, 0)

    def add_first(g, carry):
        for d in range(2):
            s1(g, d).wait_recv()
            rs = seg(-1 if d else 1)
            part_v[g, d, rs, :] = (part_v[g, d, rs, :].astype(F32) + r1_v[g, d].astype(F32)).astype(BF)
            s2(g, d, d).start()
        return carry

    with jax.named_scope('add_first'):
        lax.fori_loop(0, GROUPS, add_first, 0)

    def add_last(g, carry):
        for d in range(2):
            for half in range(2):
                s2(g, d, half).wait_recv()
        for half in range(2):
            c0 = pl.multiple_of((2 * g + half) * half_cols, half_cols)
            attn = part_v[g, half, seg(0), :].astype(F32) + r2_v[g, 0, half].astype(F32) + r2_v[g, 1, half].astype(F32)
            out_v[seg(0), pl.ds(c0, half_cols)] = (x_v[seg(0), pl.ds(c0, half_cols)].astype(F32) + attn).astype(BF)
        for d in range(2):
            f1(g, d).start()
        return carry

    with jax.named_scope('add_last'):
        lax.fori_loop(0, GROUPS, add_last, 0)

    def pass_on(g, carry):
        for d in range(2):
            f1(g, d, 1 if d else -1).wait_recv()
            f2(g, d, 1 if d else -1).start()
        return carry

    with jax.named_scope('caches'):
        k_out[...] = kc_v[...].reshape(k_out.shape)
        v_out[...] = vc_v[...].reshape(v_out.shape)

    with jax.named_scope('pass_on'):
        lax.fori_loop(0, GROUPS, pass_on, 0)

    def finish(g, carry):
        for d in range(2):
            f2(g, d, 2).wait_recv()
        return carry

    with jax.named_scope('finish'):
        lax.fori_loop(0, GROUPS, finish, 0)

    def drain(g, carry):
        for d in range(2):
            s1(g, d).wait_send()
            for half in range(2):
                s2(g, d, half).wait_send()
            f1(g, d).wait_send()
            f2(g, d, 1 if d else -1).wait_send()
        return carry

    with jax.named_scope('drain'):
        lax.fori_loop(0, GROUPS, drain, 0)

    @pl.when(core == 0)
    def _():
        own_to(0, 1, 0, sibling).wait_send()
        own_to(0, 1, 1, sibling).wait_send()

    @pl.when(right_sends)
    def _():
        own_to(1, 0, 1, x_right).wait_send()
        own_to(1, 0, 0, x_right).wait_send()

    @pl.when(left_h0_sends)
    def _():
        own_to(2, 0, 0, x_left).wait_send()

    @pl.when(left_h1_sends)
    def _():
        own_to(2, 0, 1, x_left).wait_send()

    @pl.when(has_left)
    def _():
        fwd_sib(1, 0).wait_send()
        fwd_sib(1, 1).wait_send()

    @pl.when(has_right)
    def _():
        fwd_sib(2, 0).wait_send()
        fwd_sib(2, 1).wait_send()

    @pl.when(has_far)
    def _():
        fwd_sib(3, 0).wait_send()
        fwd_sib(3, 1).wait_send()

    @pl.when(fwd_right)
    def _():
        fwd_far(1).wait_send()

    @pl.when(fwd_left)
    def _():
        fwd_far(0).wait_send()


def solution(mesh):
    ring = mesh.shape['tp']
    if mesh.shape['cp'] != 2 * ring or ring != 4:
        raise ValueError('mesh')
    row_spec = P(('dp', 'cp'), None)
    cache_spec = P(('dp', 'cp'), 'tp', None)
    head_cols = P(None, 'tp')

    def local_block(hidden, positions, norm_gain, w_query, w_key, w_value, w_out):
        rows, width = hidden.shape
        kv_heads = w_key.shape[1] // HEAD
        q_heads = w_query.shape[1] // HEAD
        seg_rows, half_cols = rows // ring, width // (2 * GROUPS)
        dma = pltpu.SemaphoreType.DMA
        out, k_new, v_new = pl.pallas_call(
            lambda *refs: block_kernel(ring, kv_heads, q_heads // kv_heads, *refs),
            out_shape=(
                pltpu.VMEM((rows, width), BF),
                pltpu.VMEM((rows, kv_heads, HEAD), BF),
                pltpu.VMEM((rows, kv_heads, HEAD), BF),
            ),
            in_specs=[pl.BlockSpec(memory_space=pl.ANY)] + [pl.BlockSpec(memory_space=pltpu.VMEM)] * 3
            + [pl.BlockSpec(memory_space=pl.ANY)] * 4,
            out_specs=[pl.BlockSpec(memory_space=pltpu.VMEM)] * 3,
            scratch_shapes=[
                pltpu.VMEM((rows, width), BF),
                pltpu.VMEM((rows, width), BF),
                pltpu.VMEM(w_query.shape, BF),
                pltpu.VMEM((width, 2 * kv_heads * HEAD), BF),
                pltpu.VMEM(w_out.shape, BF),
                pltpu.VMEM((rows, HEAD), F32),
                pltpu.VMEM((rows, HEAD), F32),
                pltpu.VMEM((rows, kv_heads * HEAD), BF),
                pltpu.VMEM((rows, kv_heads * HEAD), BF),
                pltpu.VMEM((q_heads, HEAD, rows), BF),
                pltpu.VMEM((4, 2, kv_heads, 2, rows, HEAD), BF),
                pltpu.VMEM((q_heads, 1, rows), F32),
                pltpu.VMEM((q_heads, 1, rows), F32),
                pltpu.VMEM((q_heads, HEAD, rows), F32),
                pltpu.VMEM((rows, q_heads * HEAD), BF),
                pltpu.VMEM((GROUPS, 2, rows, half_cols), BF),
                pltpu.VMEM((GROUPS, 2, seg_rows, half_cols), BF),
                pltpu.VMEM((GROUPS, 2, 2, seg_rows, half_cols), BF),
                dma((4 + LOAD_CHUNKS,)),
                dma((4, kv_heads)),
                dma((4, 2, kv_heads)),
                dma((4, kv_heads)),
                dma((GROUPS, 2)), dma((GROUPS, 2)),
                dma((GROUPS, 2, 2)), dma((GROUPS, 2, 2)),
                dma((GROUPS, 2)), dma((GROUPS, 2)),
                dma((GROUPS, 2)), dma((GROUPS, 2)),
            ],
            compiler_params=pltpu.CompilerParams(collective_id=0, has_side_effects=True, vmem_limit_bytes=60 * 1024 * 1024),
            name='attn_block',
        )(hidden, positions, norm_gain, jnp.asarray(inverse_freq()), w_query, w_key, w_value, w_out)
        return out, k_new, v_new

    return jax.shard_map(local_block, mesh=mesh,
                         in_specs=(row_spec, P(('dp', 'cp')), P(None), head_cols, head_cols, head_cols, P('tp', None)),
                         out_specs=(row_spec, cache_spec, cache_spec), check_vma=False)
```

time: 120 us -> 95.8 us (0.80)
  the two profiles are of different devices: /device:TPU:103 before, /device:TPU:102 now
where the time goes in v2:
time: 95.8 us; the launch traced here: 95.2 us
  Pallas kernels  91.5 us (96%)
  local copies, waits for them, and re-layouts  3.07 us (3%)
    pallas_call x1, Pallas kernels, local_block(): pl.pallas_call(lambda *refs: block_kernel(ring, kv_heads, q_heads // kv_h...  91.5 us
    unnamed x3, local copies, waits for them, and re-layouts  3.07 us

profile of v2, /device:TPU:102, one launch (start us, length us, event | category | flops | bytes accessed | tf_op | source)
XLA Modules:
  0.0 95.2 jit_solution(1470867679732299407)
XLA Ops:
  0.6 91.5 %attn_block.1 = (bf16[512,3072]{1,0:T(8,128)(2,1)S(1)}, bf16[512,2,128]{2,1,0:T(2,128)(2,1)S(1)}, bf16[512,2,128]{2,1,0:T(2,128)(2,1)S(1)}) custom-call(bf16[512,3072]{1,0:T(8,128)(2,1)} %refs_0_.1, s32[512]{0:T(512)} %refs_1_.1, bf16[3072]{0:T(1024)(128)(2,1)} %refs_2_.1, f32[1,128]{1,0:T(1,128)} %constant.2.clone.refs_3_, bf16[3072,768]{1,0:T(8,128)(2,1)} %refs_4_.1, ...), custom_call_target="tpu_custom_call" | custom-call | tf_op jit(solution)/shard_map/attn_block/pallas_call | solution.py:453
  92.2 1.7 %copy.14 = bf16[512,3072]{1,0:T(8,128)(2,1)} copy(bf16[512,3072]{1,0:T(8,128)(2,1)S(1)} %get-tuple-element.3) | data formatting | bytes 6291456
  93.8 0.7 copy.15
  94.5 0.7 copy.16

commit v3 on v2

--- a/solution.py
+++ b/solution.py
@@ -13,7 +13,7 @@
 SCORE_EXP2 = math.log2(math.e) / math.sqrt(HEAD)
 BF = jnp.bfloat16
 F32 = jnp.float32
-GROUPS = 6
+CHUNKS = 3
 Q_TILE = 256
 NORM_ROWS = 32
 LOAD_CHUNKS = 4
@@ -28,22 +28,27 @@
                  x_hbm, pos_ref, gain_ref, freq_ref, wq_hbm, wk_hbm, wv_hbm, wo_hbm,
                  out_v, k_out, v_out,
                  x_v, h_v, wq_v, wkv_v, wo_v, cos_v, sin_v, kc_v, vc_v, q_v, kv_v, m_v, l_v, acc_v, o_v,
-                 part_v, r1_v, r2_v,
+                 wox_v, ox_v, part_v, recv_v,
                  load_sem, kv_send, kv_recv, kv_fwd_send,
-                 s1_send, s1_recv, s2_send, s2_recv, f1_send, f1_recv, f2_send, f2_recv):
+                 wo_send, wo_recv, wo_fwd_send, wo_fwd_recv, o_send, o_recv, part_send, part_recv,
+                 f1_send, f1_recv, f2_send, f2_recv):
     rows, width = x_v.shape
     cp = lax.axis_index('cp')
     tp = lax.axis_index('tp')
     chip = cp // 2
     core = cp % 2
     seg_rows = rows // ring
-    half_cols = width // (2 * GROUPS)
+    half = width // 2
+    cols = half // CHUNKS
+    k_half = wo_v.shape[0] // 2
 
     x_right = {'cp': ((chip + 1) % ring) * 2 + core}
     x_left = {'cp': ((chip + ring - 1) % ring) * 2 + core}
     sibling = {'cp': chip * 2 + 1 - core}
     y_right = {'tp': (tp + 1) % ring}
     y_left = {'tp': (tp + ring - 1) % ring}
+    turn = 1 - 2 * (tp % 2)
+    y_mate = ({'tp': (tp + ring + turn) % ring}, {'tp': (tp + ring - turn) % ring})
 
     kv_cols = kv_heads * HEAD
     chunk = rows // LOAD_CHUNKS
@@ -71,6 +76,25 @@
             cos_v[i * HEAD:(i + 1) * HEAD, :] = jnp.cos(angles)
             sin_v[i * HEAD:(i + 1) * HEAD, :] = jnp.sin(angles) * sign
 
+    def remote(src, dst, send, recv, peer):
+        return pltpu.make_async_remote_copy(src_ref=src, dst_ref=dst, send_sem=send, recv_sem=recv,
+                                            device_id=peer, device_id_type=pl.DeviceIdType.MESH)
+
+    with jax.named_scope('barrier'):
+        pl.semaphore_wait(barrier, 5)
+
+    def wo_part(c):
+        return remote(wo_hbm.at[pl.ds(pl.multiple_of(core * k_half, k_half), k_half), c * half:(c + 1) * half],
+                      wox_v.at[c, pl.ds(pl.multiple_of(core * k_half, k_half), k_half), :],
+                      wo_send.at[c], wo_recv.at[c], y_mate[c])
+
+    def wo_share(c, from_core):
+        part = wox_v.at[c, pl.ds(pl.multiple_of(from_core * k_half, k_half), k_half), :]
+        return remote(part, part, wo_fwd_send.at[c], wo_fwd_recv.at[c], sibling)
+
+    for c in range(2):
+        wo_part(c).start()
+
     def norm_step(i, carry):
         r0 = pl.multiple_of(i * NORM_ROWS, NORM_ROWS)
         xf = x_v[pl.ds(r0, NORM_ROWS), :].astype(F32)
@@ -94,21 +118,15 @@
     kv_scope.__enter__()
     kv_proj = jnp.dot(h_v[...], wkv_v[...], preferred_element_type=F32)
     for h in range(kv_heads):
-        cols = slice(h * HEAD, (h + 1) * HEAD)
-        k_head = rope(kv_proj[:, cols])
+        hc = slice(h * HEAD, (h + 1) * HEAD)
+        k_head = rope(kv_proj[:, hc])
         kv_v[0, 0, h, 0] = k_head
-        kc_v[:, cols] = k_head
+        kc_v[:, hc] = k_head
         v_head = kv_proj[:, kv_cols + h * HEAD:kv_cols + (h + 1) * HEAD].astype(BF)
-        vc_v[:, cols] = v_head
+        vc_v[:, hc] = v_head
         for j in range(rows // HEAD):
             kv_v[0, 0, h, 1, j * HEAD:(j + 1) * HEAD, :] = v_head[j * HEAD:(j + 1) * HEAD, :].T
     kv_scope.__exit__(None, None, None)
-    with jax.named_scope('barrier'):
-        pl.semaphore_wait(barrier, 5)
-
-    def remote(src, dst, send, recv, peer):
-        return pltpu.make_async_remote_copy(src_ref=src, dst_ref=dst, send_sem=send, recv_sem=recv,
-                                            device_id=peer, device_id_type=pl.DeviceIdType.MESH)
 
     def own_to(rel, cc, head, peer):
         return remote(kv_v.at[0, 0, head], kv_v.at[rel, cc, head],
@@ -160,13 +178,12 @@
     with jax.named_scope('q_proj'):
         lax.fori_loop(0, kv_heads * group_size // 2, q_step, 0)
 
-    def scores(rel, cc, head, qi, r0, keys):
-        return jnp.dot(kv_v[rel, cc, head, 0, :keys, :], q_v[qi, :, r0:r0 + Q_TILE], preferred_element_type=F32)
-
     def attend(tiles, first):
         def start(tile):
-            rel, cc, head, qi, r0 = tile
-            s = scores(rel, cc, head, qi, r0, r0 + Q_TILE if first else rows)
+            rel, ccs, head, qi, rs, r0 = tile
+            keys = r0 + Q_TILE if first else rows
+            q_t = q_v[qi, :, rs]
+            s = jnp.concatenate([jnp.dot(kv_v[rel, cc, head, 0, :keys, :], q_t, preferred_element_type=F32) for cc in ccs], axis=0)
             if first:
                 key_id = lax.broadcasted_iota(jnp.int32, s.shape, 0)
                 row_id = lax.broadcasted_iota(jnp.int32, s.shape, 1) + r0
@@ -174,8 +191,7 @@
             return s
 
         def soften(tile, s):
-            rel, cc, head, qi, r0 = tile
-            rs = slice(r0, r0 + Q_TILE)
+            rel, ccs, head, qi, rs, r0 = tile
             m_new = jnp.max(s, axis=0, keepdims=True)
             alpha = None
             if not first:
@@ -189,9 +205,9 @@
             return p.astype(BF), alpha
 
         def gather(tile, p, alpha):
-            rel, cc, head, qi, r0 = tile
-            rs = slice(r0, r0 + Q_TILE)
-            v_t = jnp.concatenate([kv_v[rel, cc, head, 1, j * HEAD:(j + 1) * HEAD, :] for j in range(p.shape[0] // HEAD)], axis=1)
+            rel, ccs, head, qi, rs, r0 = tile
+            keys = r0 + Q_TILE if first else rows
+            v_t = jnp.concatenate([kv_v[rel, cc, head, 1, j * HEAD:(j + 1) * HEAD, :] for cc in ccs for j in range(keys // HEAD)], axis=1)
             o_new = jnp.dot(v_t, p, preferred_element_type=F32)
             acc_v[qi, :, rs] = o_new if first else acc_v[qi, :, rs] * alpha + o_new
 
@@ -206,7 +222,8 @@
             s = s_next
 
     def head_tiles(rel, cc, head):
-        return [(rel, cc, head, head * group_size + g, rt * Q_TILE) for g in range(group_size) for rt in range(rows // Q_TILE)]
+        return [(rel, (cc,), head, head * group_size + g, slice(rt * Q_TILE, (rt + 1) * Q_TILE), rt * Q_TILE)
+                for g in range(group_size) for rt in range(rows // Q_TILE)]
 
     def own_unit(head, carry):
         attend(head_tiles(0, 0, head), True)
@@ -260,18 +277,19 @@
             own_to(2, 0, 1, x_left).wait_recv()
             fwd_sib(2, 1).start()
 
-        @pl.when(jnp.logical_and(p == 3, has_far))
-        def _():
-            fwd_far(1).wait_recv()
-            fwd_sib(3, 1).start()
-            fwd_far(0).wait_recv()
-            fwd_sib(3, 0).start()
-
         def unit(i, inner):
             cc, which = i // 2, i % 2
+
+            @pl.when(jnp.logical_and(jnp.logical_and(p == 2, i == 3), has_far))
+            def _():
+                fwd_far(1).wait_recv()
+                fwd_sib(3, 1).start()
+                fwd_far(0).wait_recv()
+                fwd_sib(3, 0).start()
+
             head = (p + which) % 2
-            rel = ((p + 2) // 3) * (1 + which) + (p // 3) * (2 - which)
-            need = ((p == 0) & (cc == 1) & (core == 1)) | ((rel == 1) & has_left) | ((rel == 2) & has_right) | ((rel == 3) & has_far)
+            rel = ((p + 1) // 2) * (1 + which)
+            need = ((p == 0) & (cc == 1) & (core == 1)) | ((rel == 1) & has_left) | ((rel == 2) & has_right)
 
             @pl.when(need & (p > 0) & (cc == 1))
             def _():
@@ -288,111 +306,147 @@
         return carry
 
     with jax.named_scope('phase'):
-        lax.fori_loop(0, 4, phase, 0)
-
-    def norm_out(qi, carry):
-        c0 = pl.multiple_of(qi * HEAD, HEAD)
-        o_v[:, pl.ds(c0, HEAD)] = (acc_v[qi] * (1.0 / l_v[qi])).astype(BF).T
-        return carry
-
-    with jax.named_scope('norm_out'):
-        lax.fori_loop(0, kv_heads * group_size, norm_out, 0)
+        lax.fori_loop(0, 3, phase, 0)
+
+    def seg(index):
+        return pl.ds(pl.multiple_of(index * seg_rows, seg_rows), seg_rows)
+
+    own_seg, far_seg = tp, (tp + 2) % ring
+    mate_seg = ((tp + ring + turn) % ring, (tp + ring - turn) % ring)
+
+    def o_part(c, which):
+        return remote(o_v.at[seg(mate_seg[c] if which else far_seg), :], ox_v.at[c, which],
+                      o_send.at[c, which], o_recv.at[c, which], y_mate[c])
+
+    @pl.when(has_far)
+    def _():
+        for head in range(kv_heads):
+            remote(kv_v.at[3, 0, head], kv_v.at[3, 1, head], kv_fwd_send.at[3, head], kv_recv.at[3, 1, head], sibling).wait_recv()
+
     loads[3].wait()
 
-    def seg(offset):
-        return pl.ds(pl.multiple_of(((tp + offset + ring) % ring) * seg_rows, seg_rows), seg_rows)
-
-    def s1(g, d):
-        return remote(part_v.at[g, d, seg(2), :], r1_v.at[g, d], s1_send.at[g, d], s1_recv.at[g, d],
-                      y_left if d else y_right)
-
-    def s2(g, d, half):
-        return remote(part_v.at[g, half, seg(-1 if d else 1), :], r2_v.at[g, d, half],
-                      s2_send.at[g, d, half], s2_recv.at[g, d, half], y_left if d else y_right)
-
-    def out_at(g, offset, half=None):
-        c0, cols = (2 * g * half_cols, 2 * half_cols) if half is None else ((2 * g + half) * half_cols, half_cols)
-        return out_v.at[seg(offset), pl.ds(pl.multiple_of(c0, half_cols), cols)]
-
-    def f1(g, d, offset=0):
-        return remote(out_at(g, offset), out_at(g, offset), f1_send.at[g, d], f1_recv.at[g, d],
-                      y_left if d else y_right)
-
-    def f2(g, d, offset):
-        return remote(out_at(g, offset, d), out_at(g, offset, d), f2_send.at[g, d], f2_recv.at[g, d],
-                      y_left if d else y_right)
-
-    def project(g, carry):
-        for half in range(2):
-            c0 = pl.multiple_of((2 * g + half) * half_cols, half_cols)
-            part_v[g, half] = jnp.dot(o_v[...], wo_v[:, pl.ds(c0, half_cols)], preferred_element_type=F32).astype(BF)
-        for d in range(2):
-            s1(g, d).start()
-        for d in range(2):
-            s2(g, d, 1 - d).start()
-        return carry
-
-    with jax.named_scope('project'):
-        lax.fori_loop(0, GROUPS, project, 0)
-
-    def add_first(g, carry):
-        for d in range(2):
-            s1(g, d).wait_recv()
-            rs = seg(-1 if d else 1)
-            part_v[g, d, rs, :] = (part_v[g, d, rs, :].astype(F32) + r1_v[g, d].astype(F32)).astype(BF)
-            s2(g, d, d).start()
-        return carry
-
-    with jax.named_scope('add_first'):
-        lax.fori_loop(0, GROUPS, add_first, 0)
-
-    def add_last(g, carry):
-        for d in range(2):
-            for half in range(2):
-                s2(g, d, half).wait_recv()
-        for half in range(2):
-            c0 = pl.multiple_of((2 * g + half) * half_cols, half_cols)
-            attn = part_v[g, half, seg(0), :].astype(F32) + r2_v[g, 0, half].astype(F32) + r2_v[g, 1, half].astype(F32)
-            out_v[seg(0), pl.ds(c0, half_cols)] = (x_v[seg(0), pl.ds(c0, half_cols)].astype(F32) + attn).astype(BF)
-        for d in range(2):
-            f1(g, d).start()
-        return carry
-
-    with jax.named_scope('add_last'):
-        lax.fori_loop(0, GROUPS, add_last, 0)
-
-    def pass_on(g, carry):
-        for d in range(2):
-            f1(g, d, 1 if d else -1).wait_recv()
-            f2(g, d, 1 if d else -1).start()
-        return carry
+    def seg_step(j, carry):
+        index = (tp + ring + 2 * ((3 - j) // 3) + turn * ((j % 3) % 2) - turn * (j // 2 - j // 3)) % ring
+        rs = seg(index)
+
+        @pl.when(has_far)
+        def _():
+            with jax.named_scope('far_seg'):
+                attend([(3, (0, 1), head, head * group_size + g, rs, 0) for head in range(kv_heads) for g in range(group_size)], False)
+
+        for qi in range(kv_heads * group_size):
+            o_v[rs, qi * HEAD:(qi + 1) * HEAD] = (acc_v[qi, :, rs] * (1.0 / l_v[qi, :, rs])).astype(BF).T
+
+        @pl.when(j == 0)
+        def _():
+            for c in range(2):
+                o_part(c, 0).start()
+
+        @pl.when(j == 1)
+        def _():
+            o_part(0, 1).start()
+            with jax.named_scope('wo_wait'):
+                for c in range(2):
+                    wo_part(c).wait_recv()
+                    wo_share(c, core).start()
+
+        @pl.when(j == 2)
+        def _():
+            o_part(1, 1).start()
+
+        return carry
+
+    with jax.named_scope('segs'):
+        lax.fori_loop(0, ring, seg_step, 0)
+
+    def col(c, g):
+        return pl.ds(pl.multiple_of(c * half + g * cols, cols), cols)
+
+    def two_mates(c, g, own_rows, which):
+        g0 = pl.multiple_of(g * cols, cols)
+        return (jnp.dot(o_v[seg(own_rows), :], wo_v[:, col(c, g)], preferred_element_type=F32)
+                + jnp.dot(ox_v[c, which], wox_v[c, :, pl.ds(g0, cols)], preferred_element_type=F32))
+
+    def cross(c, g):
+        return remote(part_v.at[c, g], recv_v.at[c, g], part_send.at[c, g], part_recv.at[c, g], y_mate[1 - c])
+
+    def f1(c, g, d, owner):
+        block = out_v.at[seg(owner), col(c, g)]
+        return remote(block, block, f1_send.at[c, g, d], f1_recv.at[c, g, d], y_left if d else y_right)
+
+    def f2(g, d, owner):
+        block = out_v.at[seg(owner), col(d, g)]
+        return remote(block, block, f2_send.at[g, d], f2_recv.at[g, d], y_left if d else y_right)
+
+    with jax.named_scope('mates'):
+        for c in range(2):
+            wo_share(c, 1 - core).wait_recv()
+            o_part(c, 0).wait_recv()
+
+    def project_cross(g, carry):
+        for c in range(2):
+            part_v[c, g] = two_mates(c, g, mate_seg[1 - c], 0).astype(BF)
+            cross(c, g).start()
+        return carry
+
+    with jax.named_scope('cross'):
+        lax.fori_loop(0, CHUNKS, project_cross, 0)
 
     with jax.named_scope('caches'):
         k_out[...] = kc_v[...].reshape(k_out.shape)
         v_out[...] = vc_v[...].reshape(v_out.shape)
 
+    for c in range(2):
+        o_part(c, 1).wait_recv()
+
+    def project_own(g, carry):
+        for c in range(2):
+            attn = two_mates(c, g, own_seg, 1)
+            cross(c, g).wait_recv()
+            attn = attn + recv_v[c, g].astype(F32)
+            out_v[seg(own_seg), col(c, g)] = (x_v[seg(own_seg), col(c, g)].astype(F32) + attn).astype(BF)
+            for d in range(2):
+                f1(c, g, d, own_seg).start()
+        return carry
+
+    with jax.named_scope('own_out'):
+        lax.fori_loop(0, CHUNKS, project_own, 0)
+
+    side_seg = ((tp + ring - 1) % ring, (tp + 1) % ring)
+
+    def pass_on(g, carry):
+        for d in range(2):
+            f1(d, g, d, side_seg[d]).wait_recv()
+            f2(g, d, side_seg[d]).start()
+        return carry
+
     with jax.named_scope('pass_on'):
-        lax.fori_loop(0, GROUPS, pass_on, 0)
+        lax.fori_loop(0, CHUNKS, pass_on, 0)
 
     def finish(g, carry):
         for d in range(2):
-            f2(g, d, 2).wait_recv()
+            f1(1 - d, g, d, side_seg[d]).wait_recv()
+            f2(g, d, far_seg).wait_recv()
         return carry
 
     with jax.named_scope('finish'):
-        lax.fori_loop(0, GROUPS, finish, 0)
+        lax.fori_loop(0, CHUNKS, finish, 0)
 
     def drain(g, carry):
         for d in range(2):
-            s1(g, d).wait_send()
-            for half in range(2):
-                s2(g, d, half).wait_send()
-            f1(g, d).wait_send()
-            f2(g, d, 1 if d else -1).wait_send()
+            cross(d, g).wait_send()
+            f2(g, d, side_seg[d]).wait_send()
+            for c in range(2):
+                f1(c, g, d, own_seg).wait_send()
         return carry
 
     with jax.named_scope('drain'):
-        lax.fori_loop(0, GROUPS, drain, 0)
+        lax.fori_loop(0, CHUNKS, drain, 0)
+    for c in range(2):
+        wo_part(c).wait_send()
+        wo_share(c, core).wait_send()
+        for which in range(2):
+            o_part(c, which).wait_send()
 
     @pl.when(core == 0)
     def _():
@@ -448,7 +502,8 @@
         rows, width = hidden.shape
         kv_heads = w_key.shape[1] // HEAD
         q_heads = w_query.shape[1] // HEAD
-        seg_rows, half_cols = rows // ring, width // (2 * GROUPS)
+        seg_rows, half = rows // ring, width // 2
+        cols = half // CHUNKS
         dma = pltpu.SemaphoreType.DMA
         out, k_new, v_new = pl.pallas_call(
             lambda *refs: block_kernel(ring, kv_heads, q_heads // kv_heads, *refs),
@@ -476,17 +531,19 @@
                 pltpu.VMEM((q_heads, 1, rows), F32),
                 pltpu.VMEM((q_heads, HEAD, rows), F32),
                 pltpu.VMEM((rows, q_heads * HEAD), BF),
-                pltpu.VMEM((GROUPS, 2, rows, half_cols), BF),
-                pltpu.VMEM((GROUPS, 2, seg_rows, half_cols), BF),
-                pltpu.VMEM((GROUPS, 2, 2, seg_rows, half_cols), BF),
+                pltpu.VMEM((2, q_heads * HEAD, half), BF),
+                pltpu.VMEM((2, 2, seg_rows, q_heads * HEAD), BF),
+                pltpu.VMEM((2, CHUNKS, seg_rows, cols), BF),
+                pltpu.VMEM((2, CHUNKS, seg_rows, cols), BF),
                 dma((4 + LOAD_CHUNKS,)),
                 dma((4, kv_heads)),
                 dma((4, 2, kv_heads)),
                 dma((4, kv_heads)),
-                dma((GROUPS, 2)), dma((GROUPS, 2)),
-                dma((GROUPS, 2, 2)), dma((GROUPS, 2, 2)),
-                dma((GROUPS, 2)), dma((GROUPS, 2)),
-                dma((GROUPS, 2)), dma((GROUPS, 2)),
+                dma((2,)), dma((2,)), dma((2,)), dma((2,)),
+                dma((2, 2)), dma((2, 2)),
+                dma((2, CHUNKS)), dma((2, CHUNKS)),
+                dma((2, CHUNKS, 2)), dma((2, CHUNKS, 2)),
+                dma((CHUNKS, 2)), dma((CHUNKS, 2)),
             ],
             compiler_params=pltpu.CompilerParams(collective_id=0, has_side_effects=True, vmem_limit_bytes=60 * 1024 * 1024),
             name='attn_block',

time: 95.8 us -> 82.4 us (0.86)
  Pallas kernels: 91.5 us -> 78.5 us
    pallas_call x1, Pallas kernels: 91.5 us -> 78.5 us  [local_block(): pl.pallas_call(lambda *refs: block_kernel(ring, kv_heads, q_heads // kv_h...]
where the time goes in v3:
time: 82.4 us; the launch traced here: 82.3 us
  Pallas kernels  78.5 us (95%)
  local copies, waits for them, and re-layouts  3.07 us (4%)
    pallas_call x1, Pallas kernels, local_block(): pl.pallas_call(lambda *refs: block_kernel(ring, kv_heads, q_heads // kv_h...  78.5 us
    unnamed x3, local copies, waits for them, and re-layouts  3.07 us

profile of v3, /device:TPU:102, one launch (start us, length us, event | category | flops | bytes accessed | tf_op | source)
XLA Modules:
  0.0 82.3 jit_solution(14274647578616944407)
XLA Ops:
  0.6 78.5 %attn_block.1 = (bf16[512,3072]{1,0:T(8,128)(2,1)S(1)}, bf16[512,2,128]{2,1,0:T(2,128)(2,1)S(1)}, bf16[512,2,128]{2,1,0:T(2,128)(2,1)S(1)}) custom-call(bf16[512,3072]{1,0:T(8,128)(2,1)} %refs_0_.1, s32[512]{0:T(512)} %refs_1_.1, bf16[3072]{0:T(1024)(128)(2,1)} %refs_2_.1, f32[1,128]{1,0:T(1,128)} %constant.2.clone.refs_3_, bf16[3072,768]{1,0:T(8,128)(2,1)} %refs_4_.1, ...), custom_call_target="tpu_custom_call" | custom-call | tf_op jit(solution)/shard_map/attn_block/pallas_call | solution.py:508
  79.2 1.7 %copy.14 = bf16[512,3072]{1,0:T(8,128)(2,1)} copy(bf16[512,3072]{1,0:T(8,128)(2,1)S(1)} %get-tuple-element.3) | data formatting | bytes 6291456
  80.9 0.7 copy.15
  81.6 0.7 copy.16

commit v4 on v3

--- a/solution.py
+++ b/solution.py
@@ -17,6 +17,7 @@
 Q_TILE = 256
 NORM_ROWS = 32
 LOAD_CHUNKS = 4
+SHARED_ROWS = 128
 
 
 def inverse_freq():
@@ -30,7 +31,7 @@
                  x_v, h_v, wq_v, wkv_v, wo_v, cos_v, sin_v, kc_v, vc_v, q_v, kv_v, m_v, l_v, acc_v, o_v,
                  wox_v, ox_v, part_v, recv_v,
                  load_sem, kv_send, kv_recv, kv_fwd_send,
-                 wo_send, wo_recv, wo_fwd_send, wo_fwd_recv, o_send, o_recv, part_send, part_recv,
+                 wo_send, wo_recv, wx_send, wx_recv, wf_send, wf_recv, wo_fwd_send, wo_fwd_recv, o_send, o_recv, part_send, part_recv,
                  f1_send, f1_recv, f2_send, f2_recv):
     rows, width = x_v.shape
     cp = lax.axis_index('cp')
@@ -60,7 +61,7 @@
         pltpu.make_async_copy(wq_hbm, wq_v, load_sem.at[2]),
         pltpu.make_async_copy(wo_hbm, wo_v, load_sem.at[3]),
     ]
-    for copy in x_loads + loads[:2]:
+    for copy in x_loads[:1] + loads[:2] + x_loads[1:] + loads[2:3]:
         copy.start()
 
     barrier = pltpu.get_barrier_semaphore()
@@ -83,17 +84,36 @@
     with jax.named_scope('barrier'):
         pl.semaphore_wait(barrier, 5)
 
-    def wo_part(c):
-        return remote(wo_hbm.at[pl.ds(pl.multiple_of(core * k_half, k_half), k_half), c * half:(c + 1) * half],
-                      wox_v.at[c, pl.ds(pl.multiple_of(core * k_half, k_half), k_half), :],
-                      wo_send.at[c], wo_recv.at[c], y_mate[c])
-
-    def wo_share(c, from_core):
-        part = wox_v.at[c, pl.ds(pl.multiple_of(from_core * k_half, k_half), k_half), :]
-        return remote(part, part, wo_fwd_send.at[c], wo_fwd_recv.at[c], sibling)
+    base = core * k_half
+    direct_rows = k_half - SHARED_ROWS
+    sub_rows = SHARED_ROWS // ring
+
+    def sub_at(c, index):
+        return wox_v.at[c, pl.ds(pl.multiple_of(base + direct_rows + index * sub_rows, sub_rows), sub_rows), :]
+
+    def wo_part(c, kind):
+        start, count = (base, direct_rows) if kind == 0 else (base + direct_rows + chip * sub_rows, sub_rows)
+        ks = pl.ds(pl.multiple_of(start, sub_rows), count)
+        return remote(wo_hbm.at[ks, c * half:(c + 1) * half], wox_v.at[c, ks, :],
+                      wo_send.at[c, kind], wo_recv.at[c, kind], y_mate[c])
+
+    def wx_own(d, c, index):
+        return remote(sub_at(c, index), sub_at(c, index), wx_send.at[d, c], wx_recv.at[d, c], x_left if d else x_right)
+
+    def wx_pass(c, index):
+        return remote(sub_at(c, index), sub_at(c, index), wf_send.at[c], wf_recv.at[c], x_left if c else x_right)
+
+    def wo_share(c, kind, from_core):
+        start = from_core * k_half + kind * direct_rows
+        part = wox_v.at[c, pl.ds(pl.multiple_of(start, sub_rows), SHARED_ROWS if kind else direct_rows), :]
+        return remote(part, part, wo_fwd_send.at[c, kind], wo_fwd_recv.at[c, kind], sibling)
+
+    chip_left, chip_right, chip_far = (chip + ring - 1) % ring, (chip + 1) % ring, (chip + 2) % ring
 
     for c in range(2):
-        wo_part(c).start()
+        wo_part(c, 1).start()
+    for c in range(2):
+        wo_part(c, 0).start()
 
     def norm_step(i, carry):
         r0 = pl.multiple_of(i * NORM_ROWS, NORM_ROWS)
@@ -102,34 +122,16 @@
         h_v[pl.ds(r0, NORM_ROWS), :] = (xf * inv * gain_ref[...].astype(F32).reshape(1, width)).astype(BF)
         return carry
 
-    with jax.named_scope('norm'):
-        for i in range(LOAD_CHUNKS):
-            x_loads[i].wait()
-            lax.fori_loop(i * chunk // NORM_ROWS, (i + 1) * chunk // NORM_ROWS, norm_step, 0)
-    for copy in loads[2:]:
-        copy.start()
-
-    def rope(vals):
-        return (vals * cos_v[...] + pltpu.roll(vals, HEAD // 2, 1) * sin_v[...]).astype(BF)
-
-    for copy in loads[:2]:
-        copy.wait()
-    kv_scope = jax.named_scope('kv_proj')
-    kv_scope.__enter__()
-    kv_proj = jnp.dot(h_v[...], wkv_v[...], preferred_element_type=F32)
-    for h in range(kv_heads):
-        hc = slice(h * HEAD, (h + 1) * HEAD)
-        k_head = rope(kv_proj[:, hc])
-        kv_v[0, 0, h, 0] = k_head
-        kc_v[:, hc] = k_head
-        v_head = kv_proj[:, kv_cols + h * HEAD:kv_cols + (h + 1) * HEAD].astype(BF)
-        vc_v[:, hc] = v_head
-        for j in range(rows // HEAD):
-            kv_v[0, 0, h, 1, j * HEAD:(j + 1) * HEAD, :] = v_head[j * HEAD:(j + 1) * HEAD, :].T
-    kv_scope.__exit__(None, None, None)
+    def rope(vals, rs=slice(None)):
+        return (vals * cos_v[rs, :] + pltpu.roll(vals, HEAD // 2, 1) * sin_v[rs, :]).astype(BF)
 
     def own_to(rel, cc, head, peer):
         return remote(kv_v.at[0, 0, head], kv_v.at[rel, cc, head],
+                      kv_send.at[rel, head], kv_recv.at[rel, cc, head], peer)
+
+    def own_chunk(rel, cc, head, peer, i):
+        ks = slice(i * chunk, (i + 1) * chunk)
+        return remote(kv_v.at[0, 0, head, :, ks, :], kv_v.at[rel, cc, head, :, ks, :],
                       kv_send.at[rel, head], kv_recv.at[rel, cc, head], peer)
 
     def fwd_far(head):
@@ -145,6 +147,36 @@
     left_h0_sends = chip < 2
     left_h1_sends = chip < 1
 
+
+    for i in range(LOAD_CHUNKS):
+        x_loads[i].wait()
+        with jax.named_scope('norm'):
+            lax.fori_loop(i * chunk // NORM_ROWS, (i + 1) * chunk // NORM_ROWS, norm_step, 0)
+        if i == 0:
+            for copy in loads[:2]:
+                copy.wait()
+        ks = slice(i * chunk, (i + 1) * chunk)
+        with jax.named_scope('kv_proj'):
+            kv_proj = jnp.dot(h_v[ks, :], wkv_v[...], preferred_element_type=F32)
+            for h in range(kv_heads):
+                hc = slice(h * HEAD, (h + 1) * HEAD)
+                k_head = rope(kv_proj[:, hc], ks)
+                kv_v[0, 0, h, 0, ks, :] = k_head
+                kc_v[ks, hc] = k_head
+                v_head = kv_proj[:, kv_cols + h * HEAD:kv_cols + (h + 1) * HEAD].astype(BF)
+                vc_v[ks, hc] = v_head
+                kv_v[0, 0, h, 1, ks, :] = v_head.T
+
+        @pl.when(right_sends)
+        def _(i=i):
+            own_chunk(1, 0, 1, x_right, i).start()
+
+        @pl.when(left_h0_sends)
+        def _(i=i):
+            own_chunk(2, 0, 0, x_left, i).start()
+
+    loads[3].start()
+
     @pl.when(core == 0)
     def _():
         own_to(0, 1, 0, sibling).start()
@@ -152,14 +184,6 @@
 
     @pl.when(right_sends)
     def _():
-        own_to(1, 0, 1, x_right).start()
-
-    @pl.when(left_h0_sends)
-    def _():
-        own_to(2, 0, 0, x_left).start()
-
-    @pl.when(right_sends)
-    def _():
         own_to(1, 0, 0, x_right).start()
 
     @pl.when(left_h1_sends)
@@ -168,15 +192,15 @@
 
     loads[2].wait()
 
-    def q_step(j, carry):
-        c0 = pl.multiple_of(j * 2 * HEAD, 2 * HEAD)
-        q_proj = jnp.dot(h_v[...], wq_v[:, pl.ds(c0, 2 * HEAD)], preferred_element_type=F32)
-        q_v[2 * j] = rope(q_proj[:, :HEAD]).T
-        q_v[2 * j + 1] = rope(q_proj[:, HEAD:]).T
-        return carry
-
     with jax.named_scope('q_proj'):
-        lax.fori_loop(0, kv_heads * group_size // 2, q_step, 0)
+        q_pair = None
+        for j in range(kv_heads * group_size // 2 + 1):
+            last = q_pair
+            if j < kv_heads * group_size // 2:
+                q_pair = jnp.dot(h_v[...], wq_v[:, j * 2 * HEAD:(j + 1) * 2 * HEAD], preferred_element_type=F32)
+            if j > 0:
+                q_v[2 * j - 2] = rope(last[:, :HEAD]).T
+                q_v[2 * j - 1] = rope(last[:, HEAD:]).T
 
     def attend(tiles, first):
         def start(tile):
@@ -221,20 +245,20 @@
                 held = soften(tiles[i], s)
             s = s_next
 
-    def head_tiles(rel, cc, head):
-        return [(rel, (cc,), head, head * group_size + g, slice(rt * Q_TILE, (rt + 1) * Q_TILE), rt * Q_TILE)
+    def head_tiles(rel, ccs, head):
+        return [(rel, ccs, head, head * group_size + g, slice(rt * Q_TILE, (rt + 1) * Q_TILE), rt * Q_TILE)
                 for g in range(group_size) for rt in range(rows // Q_TILE)]
 
     def own_unit(head, carry):
-        attend(head_tiles(0, 0, head), True)
+        attend(head_tiles(0, (0,), head), True)
         return carry
 
     with jax.named_scope('own'):
         lax.fori_loop(0, kv_heads, own_unit, 0)
 
-    def far_unit(rel, cc, head):
+    def far_unit(rel, ccs, head):
         with jax.named_scope('far'):
-            attend(head_tiles(rel, cc, head), False)
+            attend(head_tiles(rel, ccs, head), False)
 
     has_left = chip >= 1
     has_right = chip >= 3
@@ -242,71 +266,42 @@
     fwd_right = jnp.logical_and(chip >= 1, chip <= 2)
     fwd_left = jnp.logical_or(chip == 0, chip == 3)
 
-    def phase(p, carry):
-        @pl.when(jnp.logical_and(p == 0, core == 1))
-        def _():
-            own_to(0, 1, 0, sibling).wait_recv()
-            own_to(0, 1, 1, sibling).wait_recv()
-
-        @pl.when(jnp.logical_and(p == 1, has_left))
-        def _():
-            own_to(1, 0, 1, x_right).wait_recv()
-
-            @pl.when(fwd_right)
-            def _():
-                fwd_far(1).start()
-
-            fwd_sib(1, 1).start()
-
-        @pl.when(jnp.logical_and(p == 1, fwd_left))
-        def _():
-            own_to(2, 0, 0, x_left).wait_recv()
-            fwd_far(0).start()
-
-            @pl.when(has_right)
-            def _():
-                fwd_sib(2, 0).start()
-
-        @pl.when(jnp.logical_and(p == 2, has_left))
-        def _():
-            own_to(1, 0, 0, x_right).wait_recv()
-            fwd_sib(1, 0).start()
-
-        @pl.when(jnp.logical_and(p == 2, has_right))
-        def _():
-            own_to(2, 0, 1, x_left).wait_recv()
-            fwd_sib(2, 1).start()
-
-        def unit(i, inner):
-            cc, which = i // 2, i % 2
-
-            @pl.when(jnp.logical_and(jnp.logical_and(p == 2, i == 3), has_far))
-            def _():
-                fwd_far(1).wait_recv()
-                fwd_sib(3, 1).start()
-                fwd_far(0).wait_recv()
-                fwd_sib(3, 0).start()
-
-            head = (p + which) % 2
-            rel = ((p + 1) // 2) * (1 + which)
-            need = ((p == 0) & (cc == 1) & (core == 1)) | ((rel == 1) & has_left) | ((rel == 2) & has_right)
-
-            @pl.when(need & (p > 0) & (cc == 1))
-            def _():
-                remote(kv_v.at[rel, 0, head], kv_v.at[rel, 1, head], kv_fwd_send.at[rel, head],
-                       kv_recv.at[rel, 1, head], sibling).wait_recv()
-
-            @pl.when(need)
-            def _():
-                far_unit(rel, cc, head)
-
-            return inner
-
-        lax.fori_loop(0, 4, unit, 0)
-        return carry
-
-    with jax.named_scope('phase'):
-        lax.fori_loop(0, 3, phase, 0)
+    @pl.when(core == 1)
+    def _():
+        own_to(0, 1, 0, sibling).wait_recv()
+        own_to(0, 1, 1, sibling).wait_recv()
+
+    @pl.when(has_left)
+    def _():
+        own_to(1, 0, 1, x_right).wait_recv()
+
+        @pl.when(fwd_right)
+        def _():
+            fwd_far(1).start()
+
+        fwd_sib(1, 1).start()
+
+    @pl.when(fwd_left)
+    def _():
+        own_to(2, 0, 0, x_left).wait_recv()
+        fwd_far(0).start()
+
+        @pl.when(has_right)
+        def _():
+            fwd_sib(2, 0).start()
+
+    for c in range(2):
+        wo_part(c, 1).wait_recv()
+        for d in range(2):
+            wx_own(d, c, chip).start()
+
+    def sibling_unit(head, carry):
+        far_unit(0, (1,), head)
+        return carry
+
+    @pl.when(core == 1)
+    def _():
+        lax.fori_loop(0, kv_heads, sibling_unit, 0)
 
     def seg(index):
         return pl.ds(pl.multiple_of(index * seg_rows, seg_rows), seg_rows)
@@ -318,22 +313,94 @@
         return remote(o_v.at[seg(mate_seg[c] if which else far_seg), :], ox_v.at[c, which],
                       o_send.at[c, which], o_recv.at[c, which], y_mate[c])
 
-    @pl.when(has_far)
-    def _():
-        for head in range(kv_heads):
-            remote(kv_v.at[3, 0, head], kv_v.at[3, 1, head], kv_fwd_send.at[3, head], kv_recv.at[3, 1, head], sibling).wait_recv()
-
     loads[3].wait()
 
-    def seg_step(j, carry):
+    def sib_wait(rel, head):
+        remote(kv_v.at[rel, 0, head], kv_v.at[rel, 1, head], kv_fwd_send.at[rel, head], kv_recv.at[rel, 1, head], sibling).wait_recv()
+
+    def side_unit(i, carry):
+        @pl.when((i == 0) & has_left)
+        def _():
+            sib_wait(1, 1)
+
+        @pl.when((i == 1) & has_left)
+        def _():
+            own_to(1, 0, 0, x_right).wait_recv()
+            fwd_sib(1, 0).start()
+
+        @pl.when((i == 1) & has_right)
+        def _():
+            sib_wait(2, 0)
+            own_to(2, 0, 1, x_left).wait_recv()
+            fwd_sib(2, 1).start()
+
+        @pl.when(((i == 0) & has_left) | ((i == 1) & has_right))
+        def _():
+            far_unit(1 + i, (0, 1), 1 - i)
+
+        return carry
+
+    lax.fori_loop(0, 2, side_unit, 0)
+
+    def seg_tiles(rs, *pieces):
+        return [(rel, (0, 1), head, head * group_size + g, rs, 0) for rel, head in pieces for g in range(group_size)]
+
+    def seg_step(k, carry):
+        j = (k % 2) * (1 - k // 4) + (k // 2) * (k // 4)
         index = (tp + ring + 2 * ((3 - j) // 3) + turn * ((j % 3) % 2) - turn * (j // 2 - j // 3)) % ring
         rs = seg(index)
-
-        @pl.when(has_far)
+        near = (k < 2) | (k == 4) | (k == 6)
+
+        @pl.when((k == 0) & has_left)
+        def _():
+            sib_wait(1, 0)
+
+        @pl.when((k == 0) & has_right)
+        def _():
+            sib_wait(2, 1)
+
+        @pl.when((k == 1) & has_far)
+        def _():
+            fwd_far(1).wait_recv()
+            fwd_sib(3, 1).start()
+            fwd_far(0).wait_recv()
+            fwd_sib(3, 0).start()
+
+        @pl.when((k == 2) & has_far)
+        def _():
+            sib_wait(3, 1)
+            sib_wait(3, 0)
+
+        @pl.when(k == 3)
+        def _():
+            with jax.named_scope('wx_wait'):
+                wx_own(0, 0, chip_left).wait_recv()
+                wx_pass(0, chip_left).start()
+                wx_own(1, 1, chip_right).wait_recv()
+                wx_pass(1, chip_right).start()
+
+        @pl.when(near & has_right)
+        def _():
+            with jax.named_scope('near_seg'):
+                attend(seg_tiles(rs, (1, 0), (2, 1)), False)
+
+        @pl.when(near & (has_left & (chip < 3)))
+        def _():
+            with jax.named_scope('left_seg'):
+                attend(seg_tiles(rs, (1, 0)), False)
+
+        @pl.when(jnp.logical_not(near) & has_far)
         def _():
             with jax.named_scope('far_seg'):
-                attend([(3, (0, 1), head, head * group_size + g, rs, 0) for head in range(kv_heads) for g in range(group_size)], False)
-
+                attend(seg_tiles(rs, (3, 1), (3, 0)), False)
+
+        @pl.when(jnp.logical_not(near))
+        def _():
+            seg_done(j, rs)
+
+        return carry
+
+    def seg_done(j, rs):
         for qi in range(kv_heads * group_size):
             o_v[rs, qi * HEAD:(qi + 1) * HEAD] = (acc_v[qi, :, rs] * (1.0 / l_v[qi, :, rs])).astype(BF).T
 
@@ -347,17 +414,21 @@
             o_part(0, 1).start()
             with jax.named_scope('wo_wait'):
                 for c in range(2):
-                    wo_part(c).wait_recv()
-                    wo_share(c, core).start()
+                    wo_part(c, 0).wait_recv()
+                    wo_share(c, 0, core).start()
 
         @pl.when(j == 2)
         def _():
             o_part(1, 1).start()
-
-        return carry
+            with jax.named_scope('sub_wait'):
+                wx_own(0, 1, chip_left).wait_recv()
+                wx_own(1, 0, chip_right).wait_recv()
+                for c in range(2):
+                    wx_pass(c, chip_far).wait_recv()
+                    wo_share(c, 1, core).start()
 
     with jax.named_scope('segs'):
-        lax.fori_loop(0, ring, seg_step, 0)
+        lax.fori_loop(0, 2 * ring, seg_step, 0)
 
     def col(c, g):
         return pl.ds(pl.multiple_of(c * half + g * cols, cols), cols)
@@ -380,7 +451,8 @@
 
     with jax.named_scope('mates'):
         for c in range(2):
-            wo_share(c, 1 - core).wait_recv()
+            for kind in range(2):
+                wo_share(c, kind, 1 - core).wait_recv()
             o_part(c, 0).wait_recv()
 
     def project_cross(g, carry):
@@ -443,10 +515,12 @@
     with jax.named_scope('drain'):
         lax.fori_loop(0, CHUNKS, drain, 0)
     for c in range(2):
-        wo_part(c).wait_send()
-        wo_share(c, core).wait_send()
-        for which in range(2):
-            o_part(c, which).wait_send()
+        wx_pass(c, chip_right if c else chip_left).wait_send()
+        for i in range(2):
+            wo_part(c, i).wait_send()
+            wx_own(i, c, chip).wait_send()
+            wo_share(c, i, core).wait_send()
+            o_part(c, i).wait_send()
 
     @pl.when(core == 0)
     def _():
@@ -539,7 +613,7 @@
                 dma((4, kv_heads)),
                 dma((4, 2, kv_heads)),
                 dma((4, kv_heads)),
-                dma((2,)), dma((2,)), dma((2,)), dma((2,)),
+                dma((2, 2)), dma((2, 2)), dma((2, 2)), dma((2, 2)), dma((2,)), dma((2,)), dma((2, 2)), dma((2, 2)),
                 dma((2, 2)), dma((2, 2)),
                 dma((2, CHUNKS)), dma((2, CHUNKS)),
                 dma((2, CHUNKS, 2)), dma((2, CHUNKS, 2)),

time: 82.4 us -> 80.7 us (0.979)
  Pallas kernels: 78.5 us -> 76.8 us
    pallas_call x1, Pallas kernels: 78.5 us -> 76.8 us  [local_block(): pl.pallas_call(lambda *refs: block_kernel(ring, kv_heads, q_heads // kv_h...]
where the time goes in v4:
time: 80.7 us; the launch traced here: 80.6 us
  Pallas kernels  76.8 us (95%)
  local copies, waits for them, and re-layouts  3.07 us (4%)
    pallas_call x1, Pallas kernels, local_block(): pl.pallas_call(lambda *refs: block_kernel(ring, kv_heads, q_heads // kv_h...  76.8 us
    unnamed x3, local copies, waits for them, and re-layouts  3.07 us

profile of v4, /device:TPU:102, one launch (start us, length us, event | category | flops | bytes accessed | tf_op | source)
XLA Modules:
  0.0 80.6 jit_solution(8731332155198257678)
XLA Ops:
  0.6 76.8 %attn_block.1 = (bf16[512,3072]{1,0:T(8,128)(2,1)S(1)}, bf16[512,2,128]{2,1,0:T(2,128)(2,1)S(1)}, bf16[512,2,128]{2,1,0:T(2,128)(2,1)S(1)}) custom-call(bf16[512,3072]{1,0:T(8,128)(2,1)} %refs_0_.1, s32[512]{0:T(512)} %refs_1_.1, bf16[3072]{0:T(1024)(128)(2,1)} %refs_2_.1, f32[1,128]{1,0:T(1,128)} %constant.2.clone.refs_3_, bf16[3072,768]{1,0:T(8,128)(2,1)} %refs_4_.1, ...), custom_call_target="tpu_custom_call" | custom-call | tf_op jit(solution)/shard_map/attn_block/pallas_call | solution.py:582
  77.5 1.7 %copy.14 = bf16[512,3072]{1,0:T(8,128)(2,1)} copy(bf16[512,3072]{1,0:T(8,128)(2,1)S(1)} %get-tuple-element.3) | data formatting | bytes 6291456
  79.1 0.7 copy.15
  79.9 0.7 copy.16

commit v5 on v4

--- a/solution.py
+++ b/solution.py
@@ -17,7 +17,7 @@
 Q_TILE = 256
 NORM_ROWS = 32
 LOAD_CHUNKS = 4
-SHARED_ROWS = 128
+SHARED_ROWS = 64
 
 
 def inverse_freq():
@@ -30,7 +30,7 @@
                  out_v, k_out, v_out,
                  x_v, h_v, wq_v, wkv_v, wo_v, cos_v, sin_v, kc_v, vc_v, q_v, kv_v, m_v, l_v, acc_v, o_v,
                  wox_v, ox_v, part_v, recv_v,
-                 load_sem, kv_send, kv_recv, kv_fwd_send,
+                 load_sem, kv_send, kv_recv, kv_fwd_send, far_send, far_recv,
                  wo_send, wo_recv, wx_send, wx_recv, wf_send, wf_recv, wo_fwd_send, wo_fwd_recv, o_send, o_recv, part_send, part_recv,
                  f1_send, f1_recv, f2_send, f2_recv):
     rows, width = x_v.shape
@@ -100,8 +100,8 @@
     def wx_own(d, c, index):
         return remote(sub_at(c, index), sub_at(c, index), wx_send.at[d, c], wx_recv.at[d, c], x_left if d else x_right)
 
-    def wx_pass(c, index):
-        return remote(sub_at(c, index), sub_at(c, index), wf_send.at[c], wf_recv.at[c], x_left if c else x_right)
+    def wx_pass(d, c, index):
+        return remote(sub_at(c, index), sub_at(c, index), wf_send.at[d, c], wf_recv.at[d, c], x_left if d else x_right)
 
     def wo_share(c, kind, from_core):
         start = from_core * k_half + kind * direct_rows
@@ -115,11 +115,13 @@
     for c in range(2):
         wo_part(c, 0).start()
 
+    def norm_rows(r0, count):
+        xf = x_v[pl.ds(r0, count), :].astype(F32)
+        inv = lax.rsqrt(jnp.mean(xf * xf, axis=-1, keepdims=True) + EPS)
+        h_v[pl.ds(r0, count), :] = (xf * inv * gain_ref[...].astype(F32).reshape(1, width)).astype(BF)
+
     def norm_step(i, carry):
-        r0 = pl.multiple_of(i * NORM_ROWS, NORM_ROWS)
-        xf = x_v[pl.ds(r0, NORM_ROWS), :].astype(F32)
-        inv = lax.rsqrt(jnp.mean(xf * xf, axis=-1, keepdims=True) + EPS)
-        h_v[pl.ds(r0, NORM_ROWS), :] = (xf * inv * gain_ref[...].astype(F32).reshape(1, width)).astype(BF)
+        norm_rows(pl.multiple_of(i * NORM_ROWS, NORM_ROWS), NORM_ROWS)
         return carry
 
     def rope(vals, rs=slice(None)):
@@ -129,35 +131,41 @@
         return remote(kv_v.at[0, 0, head], kv_v.at[rel, cc, head],
                       kv_send.at[rel, head], kv_recv.at[rel, cc, head], peer)
 
-    def own_chunk(rel, cc, head, peer, i):
+    def own_chunk(rel, head, peer, i):
         ks = slice(i * chunk, (i + 1) * chunk)
-        return remote(kv_v.at[0, 0, head, :, ks, :], kv_v.at[rel, cc, head, :, ks, :],
-                      kv_send.at[rel, head], kv_recv.at[rel, cc, head], peer)
-
-    def fwd_far(head):
-        rel, peer = (1, x_right) if head == 1 else (2, x_left)
-        return remote(kv_v.at[rel, 0, head], kv_v.at[3, 0, head],
-                      kv_send.at[3, head], kv_recv.at[3, 0, head], peer)
+        return remote(kv_v.at[0, 0, head, :, ks, :], kv_v.at[rel, 0, head, :, ks, :],
+                      kv_send.at[rel, head], kv_recv.at[rel, 0, head], peer)
+
+    def left_v(head, ks=slice(None)):
+        return remote(kv_v.at[0, 0, head, 1, ks, :], kv_v.at[2, 0, head, 1, ks, :],
+                      kv_send.at[2, head], kv_recv.at[2, 0, head], x_left)
+
+    def far_k(head):
+        return remote(kv_v.at[1, 0, head, 0], kv_v.at[3, 0, head, 0], far_send.at[head, 0], far_recv.at[head, 0], x_right)
+
+    def far_v(head):
+        return remote(kv_v.at[2, 0, head, 1], kv_v.at[3, 0, head, 1], far_send.at[head, 1], far_recv.at[head, 1], x_left)
 
     def fwd_sib(rel, head):
         return remote(kv_v.at[rel, 0, head], kv_v.at[rel, 1, head],
                       kv_fwd_send.at[rel, head], kv_recv.at[rel, 1, head], sibling)
 
     right_sends = chip < ring - 1
-    left_h0_sends = chip < 2
-    left_h1_sends = chip < 1
-
-
+
+    x_loads[0].wait()
+    with jax.named_scope('norm'):
+        lax.fori_loop(0, chunk // NORM_ROWS, norm_step, 0)
+    for copy in loads[:2]:
+        copy.wait()
     for i in range(LOAD_CHUNKS):
-        x_loads[i].wait()
-        with jax.named_scope('norm'):
-            lax.fori_loop(i * chunk // NORM_ROWS, (i + 1) * chunk // NORM_ROWS, norm_step, 0)
-        if i == 0:
-            for copy in loads[:2]:
-                copy.wait()
+        if i + 1 < LOAD_CHUNKS:
+            x_loads[i + 1].wait()
         ks = slice(i * chunk, (i + 1) * chunk)
         with jax.named_scope('kv_proj'):
             kv_proj = jnp.dot(h_v[ks, :], wkv_v[...], preferred_element_type=F32)
+            if i + 1 < LOAD_CHUNKS:
+                for r in range(0, chunk, 16):
+                    norm_rows((i + 1) * chunk + r, 16)
             for h in range(kv_heads):
                 hc = slice(h * HEAD, (h + 1) * HEAD)
                 k_head = rope(kv_proj[:, hc], ks)
@@ -169,11 +177,15 @@
 
         @pl.when(right_sends)
         def _(i=i):
-            own_chunk(1, 0, 1, x_right, i).start()
-
-        @pl.when(left_h0_sends)
+            own_chunk(1, 0, x_right, i).start()
+
+        @pl.when(chip == 0)
         def _(i=i):
-            own_chunk(2, 0, 0, x_left, i).start()
+            own_chunk(2, 0, x_left, i).start()
+
+        @pl.when(chip == 1)
+        def _(i=i):
+            left_v(0, slice(i * chunk, (i + 1) * chunk)).start()
 
     loads[3].start()
 
@@ -184,11 +196,15 @@
 
     @pl.when(right_sends)
     def _():
-        own_to(1, 0, 0, x_right).start()
-
-    @pl.when(left_h1_sends)
+        own_to(1, 0, 1, x_right).start()
+
+    @pl.when(chip == 0)
     def _():
         own_to(2, 0, 1, x_left).start()
+
+    @pl.when(chip == 1)
+    def _():
+        left_v(1).start()
 
     loads[2].wait()
 
@@ -264,7 +280,24 @@
     has_right = chip >= 3
     has_far = chip >= 2
     fwd_right = jnp.logical_and(chip >= 1, chip <= 2)
-    fwd_left = jnp.logical_or(chip == 0, chip == 3)
+
+    def take_left(head):
+        own_to(1, 0, head, x_right).wait_recv()
+
+        @pl.when(fwd_right)
+        def _():
+            far_k(head).start()
+
+        fwd_sib(1, head).start()
+
+    def take_right(head):
+        own_to(2, 0, head, x_left).wait_recv()
+        far_v(head).start()
+        fwd_sib(2, head).start()
+
+    def relay_right(head):
+        left_v(head).wait_recv()
+        far_v(head).start()
 
     @pl.when(core == 1)
     def _():
@@ -273,27 +306,32 @@
 
     @pl.when(has_left)
     def _():
-        own_to(1, 0, 1, x_right).wait_recv()
-
-        @pl.when(fwd_right)
-        def _():
-            fwd_far(1).start()
-
-        fwd_sib(1, 1).start()
-
-    @pl.when(fwd_left)
-    def _():
-        own_to(2, 0, 0, x_left).wait_recv()
-        fwd_far(0).start()
-
-        @pl.when(has_right)
-        def _():
-            fwd_sib(2, 0).start()
+        take_left(0)
+
+    @pl.when(has_right)
+    def _():
+        take_right(0)
+
+    @pl.when(chip == 0)
+    def _():
+        relay_right(0)
+
+    ends = jnp.logical_or(chip == 0, chip == 3)
+
+    def wx_start(d):
+        for c in range(2):
+            wx_own(d, c, chip).start()
 
     for c in range(2):
         wo_part(c, 1).wait_recv()
-        for d in range(2):
-            wx_own(d, c, chip).start()
+
+    @pl.when(ends)
+    def _():
+        wx_start(0)
+
+    @pl.when(fwd_right)
+    def _():
+        wx_start(1)
 
     def sibling_unit(head, carry):
         far_unit(0, (1,), head)
@@ -303,132 +341,164 @@
     def _():
         lax.fori_loop(0, kv_heads, sibling_unit, 0)
 
+    @pl.when(fwd_right)
+    def _():
+        take_left(1)
+
+    @pl.when(chip == 0)
+    def _():
+        relay_right(1)
+
     def seg(index):
         return pl.ds(pl.multiple_of(index * seg_rows, seg_rows), seg_rows)
 
     own_seg, far_seg = tp, (tp + 2) % ring
     mate_seg = ((tp + ring + turn) % ring, (tp + ring - turn) % ring)
 
-    def o_part(c, which):
-        return remote(o_v.at[seg(mate_seg[c] if which else far_seg), :], ox_v.at[c, which],
-                      o_send.at[c, which], o_recv.at[c, which], y_mate[c])
+    head_cols = group_size * HEAD
+
+    def o_part(c, which, head):
+        hc = slice(head * head_cols, (head + 1) * head_cols)
+        return remote(o_v.at[seg(mate_seg[c] if which else far_seg), hc], ox_v.at[c, which, :, hc],
+                      o_send.at[c, which, head], o_recv.at[c, which, head], y_mate[c])
+
+    def finish_rows(head, rs):
+        for qi in range(head * group_size, (head + 1) * group_size):
+            o_v[rs, qi * HEAD:(qi + 1) * HEAD] = (acc_v[qi, :, rs] * (1.0 / l_v[qi, :, rs])).astype(BF).T
 
     loads[3].wait()
 
     def sib_wait(rel, head):
         remote(kv_v.at[rel, 0, head], kv_v.at[rel, 1, head], kv_fwd_send.at[rel, head], kv_recv.at[rel, 1, head], sibling).wait_recv()
 
-    def side_unit(i, carry):
-        @pl.when((i == 0) & has_left)
+    def side_unit(u, carry):
+        head = (1 - u % 2) * ((u + 2) // 4)
+        rel = (1 - u % 2) * (1 + u // 4) + (u % 2) * (2 + u // 3)
+        need = ((rel == 1) & has_left) | ((rel == 2) & has_right) | ((rel == 3) & has_far)
+
+        @pl.when((u == 0) & has_left)
+        def _():
+            sib_wait(1, 0)
+
+        @pl.when((u == 1) & has_right)
+        def _():
+            take_left(1)
+            take_right(1)
+
+        @pl.when((u == 1) & fwd_right)
+        def _():
+            wx_start(0)
+
+        @pl.when((u == 1) & ends)
+        def _():
+            wx_start(1)
+
+        @pl.when((u == 1) & has_right)
+        def _():
+            sib_wait(2, 0)
+
+        @pl.when((u == 2) & (chip < 2))
+        def _():
+            with jax.named_scope('wx_wait'):
+                for d in range(2):
+                    for c in range(2):
+                        wx_own(d, c, chip_right if d else chip_left).wait_recv()
+                        wx_pass(d, c, chip_right if d else chip_left).start()
+
+        @pl.when((u == 2) & has_far)
+        def _():
+            with jax.named_scope('far_h0'):
+                far_k(0).wait_recv()
+                far_v(0).wait_recv()
+                fwd_sib(3, 0).start()
+
+        @pl.when((u == 2) & has_left)
         def _():
             sib_wait(1, 1)
 
-        @pl.when((i == 1) & has_left)
-        def _():
-            own_to(1, 0, 0, x_right).wait_recv()
-            fwd_sib(1, 0).start()
-
-        @pl.when((i == 1) & has_right)
-        def _():
-            sib_wait(2, 0)
-            own_to(2, 0, 1, x_left).wait_recv()
-            fwd_sib(2, 1).start()
-
-        @pl.when(((i == 0) & has_left) | ((i == 1) & has_right))
-        def _():
-            far_unit(1 + i, (0, 1), 1 - i)
-
-        return carry
-
-    lax.fori_loop(0, 2, side_unit, 0)
-
-    def seg_tiles(rs, *pieces):
-        return [(rel, (0, 1), head, head * group_size + g, rs, 0) for rel, head in pieces for g in range(group_size)]
-
-    def seg_step(k, carry):
-        j = (k % 2) * (1 - k // 4) + (k // 2) * (k // 4)
+        @pl.when((u == 3) & has_far)
+        def _():
+            sib_wait(3, 0)
+
+        @pl.when(u == 4)
+        def _():
+            finish_rows(0, slice(0, rows))
+            for c in range(2):
+                o_part(c, 0, 0).start()
+            for c in range(2):
+                o_part(c, 1, 0).start()
+
+        @pl.when((u == 4) & has_far)
+        def _():
+            with jax.named_scope('far_h1'):
+                far_k(1).wait_recv()
+                far_v(1).wait_recv()
+                fwd_sib(3, 1).start()
+
+        @pl.when((u == 4) & has_right)
+        def _():
+            sib_wait(2, 1)
+
+        @pl.when(need)
+        def _():
+            far_unit(rel, (0, 1), head)
+
+        return carry
+
+    lax.fori_loop(0, 5, side_unit, 0)
+
+    with jax.named_scope('wo_wait'):
+        for c in range(2):
+            wo_part(c, 0).wait_recv()
+            wo_share(c, 0, core).start()
+
+    @pl.when(has_far)
+    def _():
+        sib_wait(3, 1)
+
+    def seg_step(j, carry):
         index = (tp + ring + 2 * ((3 - j) // 3) + turn * ((j % 3) % 2) - turn * (j // 2 - j // 3)) % ring
         rs = seg(index)
-        near = (k < 2) | (k == 4) | (k == 6)
-
-        @pl.when((k == 0) & has_left)
-        def _():
-            sib_wait(1, 0)
-
-        @pl.when((k == 0) & has_right)
-        def _():
-            sib_wait(2, 1)
-
-        @pl.when((k == 1) & has_far)
-        def _():
-            fwd_far(1).wait_recv()
-            fwd_sib(3, 1).start()
-            fwd_far(0).wait_recv()
-            fwd_sib(3, 0).start()
-
-        @pl.when((k == 2) & has_far)
-        def _():
-            sib_wait(3, 1)
-            sib_wait(3, 0)
-
-        @pl.when(k == 3)
-        def _():
-            with jax.named_scope('wx_wait'):
-                wx_own(0, 0, chip_left).wait_recv()
-                wx_pass(0, chip_left).start()
-                wx_own(1, 1, chip_right).wait_recv()
-                wx_pass(1, chip_right).start()
-
-        @pl.when(near & has_right)
-        def _():
-            with jax.named_scope('near_seg'):
-                attend(seg_tiles(rs, (1, 0), (2, 1)), False)
-
-        @pl.when(near & (has_left & (chip < 3)))
-        def _():
-            with jax.named_scope('left_seg'):
-                attend(seg_tiles(rs, (1, 0)), False)
-
-        @pl.when(jnp.logical_not(near) & has_far)
+
+        @pl.when(has_far)
         def _():
             with jax.named_scope('far_seg'):
-                attend(seg_tiles(rs, (3, 1), (3, 0)), False)
-
-        @pl.when(jnp.logical_not(near))
-        def _():
-            seg_done(j, rs)
-
-        return carry
-
-    def seg_done(j, rs):
-        for qi in range(kv_heads * group_size):
-            o_v[rs, qi * HEAD:(qi + 1) * HEAD] = (acc_v[qi, :, rs] * (1.0 / l_v[qi, :, rs])).astype(BF).T
+                attend([(3, (0, 1), 1, group_size + g, rs, 0) for g in range(group_size)], False)
+
+        finish_rows(1, rs)
 
         @pl.when(j == 0)
         def _():
             for c in range(2):
-                o_part(c, 0).start()
+                o_part(c, 0, 1).start()
 
         @pl.when(j == 1)
         def _():
-            o_part(0, 1).start()
-            with jax.named_scope('wo_wait'):
+            o_part(0, 1, 1).start()
+
+        @pl.when(j == 2)
+        def _():
+            o_part(1, 1, 1).start()
+            with jax.named_scope('sub_wait'):
+                @pl.when(has_far)
+                def _():
+                    for d in range(2):
+                        for c in range(2):
+                            wx_own(d, c, chip_right if d else chip_left).wait_recv()
+
+                for d, gets in ((0, fwd_right), (1, ends)):
+                    @pl.when(gets)
+                    def _(d=d):
+                        for c in range(2):
+                            wx_pass(d, c, chip_far).wait_recv()
+
                 for c in range(2):
-                    wo_part(c, 0).wait_recv()
-                    wo_share(c, 0, core).start()
-
-        @pl.when(j == 2)
-        def _():
-            o_part(1, 1).start()
-            with jax.named_scope('sub_wait'):
-                wx_own(0, 1, chip_left).wait_recv()
-                wx_own(1, 0, chip_right).wait_recv()
-                for c in range(2):
-                    wx_pass(c, chip_far).wait_recv()
                     wo_share(c, 1, core).start()
 
+        return carry
+
     with jax.named_scope('segs'):
-        lax.fori_loop(0, 2 * ring, seg_step, 0)
+        lax.fori_loop(0, ring, seg_step, 0)
 
     def col(c, g):
         return pl.ds(pl.multiple_of(c * half + g * cols, cols), cols)
@@ -453,7 +523,8 @@
         for c in range(2):
             for kind in range(2):
                 wo_share(c, kind, 1 - core).wait_recv()
-            o_part(c, 0).wait_recv()
+            for head in range(kv_heads):
+                o_part(c, 0, head).wait_recv()
 
     def project_cross(g, carry):
         for c in range(2):
@@ -469,7 +540,8 @@
         v_out[...] = vc_v[...].reshape(v_out.shape)
 
     for c in range(2):
-        o_part(c, 1).wait_recv()
+        for head in range(kv_heads):
+            o_part(c, 1, head).wait_recv()
 
     def project_own(g, carry):
         for c in range(2):
@@ -515,53 +587,48 @@
     with jax.named_scope('drain'):
         lax.fori_loop(0, CHUNKS, drain, 0)
     for c in range(2):
-        wx_pass(c, chip_right if c else chip_left).wait_send()
+        @pl.when(chip < 2)
+        def _(c=c):
+            for d in range(2):
+                wx_pass(d, c, chip_right if d else chip_left).wait_send()
+
         for i in range(2):
             wo_part(c, i).wait_send()
             wx_own(i, c, chip).wait_send()
             wo_share(c, i, core).wait_send()
-            o_part(c, i).wait_send()
+            for head in range(kv_heads):
+                o_part(c, i, head).wait_send()
 
     @pl.when(core == 0)
     def _():
         own_to(0, 1, 0, sibling).wait_send()
         own_to(0, 1, 1, sibling).wait_send()
 
-    @pl.when(right_sends)
-    def _():
-        own_to(1, 0, 1, x_right).wait_send()
-        own_to(1, 0, 0, x_right).wait_send()
-
-    @pl.when(left_h0_sends)
-    def _():
-        own_to(2, 0, 0, x_left).wait_send()
-
-    @pl.when(left_h1_sends)
-    def _():
-        own_to(2, 0, 1, x_left).wait_send()
-
-    @pl.when(has_left)
-    def _():
-        fwd_sib(1, 0).wait_send()
-        fwd_sib(1, 1).wait_send()
-
-    @pl.when(has_right)
-    def _():
-        fwd_sib(2, 0).wait_send()
-        fwd_sib(2, 1).wait_send()
-
-    @pl.when(has_far)
-    def _():
-        fwd_sib(3, 0).wait_send()
-        fwd_sib(3, 1).wait_send()
-
-    @pl.when(fwd_right)
-    def _():
-        fwd_far(1).wait_send()
-
-    @pl.when(fwd_left)
-    def _():
-        fwd_far(0).wait_send()
+    for head in range(kv_heads):
+        @pl.when(right_sends)
+        def _(head=head):
+            own_to(1, 0, head, x_right).wait_send()
+
+        @pl.when(chip == 0)
+        def _(head=head):
+            own_to(2, 0, head, x_left).wait_send()
+
+        @pl.when(chip == 1)
+        def _(head=head):
+            left_v(head).wait_send()
+
+        @pl.when(fwd_right)
+        def _(head=head):
+            far_k(head).wait_send()
+
+        @pl.when(jnp.logical_or(chip == 0, has_right))
+        def _(head=head):
+            far_v(head).wait_send()
+
+        for rel, sent in ((1, has_left), (2, has_right), (3, has_far)):
+            @pl.when(sent)
+            def _(rel=rel, head=head):
+                fwd_sib(rel, head).wait_send()
 
 
 def solution(mesh):
@@ -610,11 +677,12 @@
                 pltpu.VMEM((2, CHUNKS, seg_rows, cols), BF),
                 pltpu.VMEM((2, CHUNKS, seg_rows, cols), BF),
                 dma((4 + LOAD_CHUNKS,)),
-                dma((4, kv_heads)),
+                dma((3, kv_heads)),
                 dma((4, 2, kv_heads)),
                 dma((4, kv_heads)),
-                dma((2, 2)), dma((2, 2)), dma((2, 2)), dma((2, 2)), dma((2,)), dma((2,)), dma((2, 2)), dma((2, 2)),
-                dma((2, 2)), dma((2, 2)),
+                dma((kv_heads, 2)), dma((kv_heads, 2)),
+                dma((2, 2)), dma((2, 2)), dma((2, 2)), dma((2, 2)), dma((2, 2)), dma((2, 2)), dma((2, 2)), dma((2, 2)),
+                dma((2, 2, kv_heads)), dma((2, 2, kv_heads)),
                 dma((2, CHUNKS)), dma((2, CHUNKS)),
                 dma((2, CHUNKS, 2)), dma((2, CHUNKS, 2)),
                 dma((CHUNKS, 2)), dma((CHUNKS, 2)),

time: 80.7 us -> 78.4 us (0.971)
  Pallas kernels: 76.8 us -> 74 us
    pallas_call x1, Pallas kernels: 76.8 us -> 74 us  [local_block(): pl.pallas_call(lambda *refs: block_kernel(ring, kv_heads, q_heads // kv_h...]
where the time goes in v5:
time: 78.4 us; the launch traced here: 77.7 us
  Pallas kernels  74 us (94%)
  local copies, waits for them, and re-layouts  3.07 us (4%)
    pallas_call x1, Pallas kernels, local_block(): pl.pallas_call(lambda *refs: block_kernel(ring, kv_heads, q_heads // kv_h...  74 us
    unnamed x3, local copies, waits for them, and re-layouts  3.07 us

profile of v5, /device:TPU:102, one launch (start us, length us, event | category | flops | bytes accessed | tf_op | source)
XLA Modules:
  0.0 77.7 jit_solution(10438918393970227422)
XLA Ops:
  0.6 74.0 %attn_block.1 = (bf16[512,3072]{1,0:T(8,128)(2,1)S(1)}, bf16[512,2,128]{2,1,0:T(2,128)(2,1)S(1)}, bf16[512,2,128]{2,1,0:T(2,128)(2,1)S(1)}) custom-call(bf16[512,3072]{1,0:T(8,128)(2,1)} %refs_0_.1, s32[512]{0:T(512)} %refs_1_.1, bf16[3072]{0:T(1024)(128)(2,1)} %refs_2_.1, f32[1,128]{1,0:T(1,128)} %constant.2.clone.refs_3_, bf16[3072,768]{1,0:T(8,128)(2,1)} %refs_4_.1, ...), custom_call_target="tpu_custom_call" | custom-call | tf_op jit(solution)/shard_map/attn_block/pallas_call | solution.py:649
  74.6 1.7 %copy.14 = bf16[512,3072]{1,0:T(8,128)(2,1)} copy(bf16[512,3072]{1,0:T(8,128)(2,1)S(1)} %get-tuple-element.3) | data formatting | bytes 6291456
  76.3 0.7 copy.15
  77.0 0.7 copy.16

commit v6 on v5

--- a/solution.py
+++ b/solution.py
@@ -17,7 +17,7 @@
 Q_TILE = 256
 NORM_ROWS = 32
 LOAD_CHUNKS = 4
-SHARED_ROWS = 64
+SHARED_ROWS = 96
 
 
 def inverse_freq():
@@ -30,7 +30,7 @@
                  out_v, k_out, v_out,
                  x_v, h_v, wq_v, wkv_v, wo_v, cos_v, sin_v, kc_v, vc_v, q_v, kv_v, m_v, l_v, acc_v, o_v,
                  wox_v, ox_v, part_v, recv_v,
-                 load_sem, kv_send, kv_recv, kv_fwd_send, far_send, far_recv,
+                 load_sem, kv_send, kv_recv, kv_fwd_send, far_send, far_recv, late_recv,
                  wo_send, wo_recv, wx_send, wx_recv, wf_send, wf_recv, wo_fwd_send, wo_fwd_recv, o_send, o_recv, part_send, part_recv,
                  f1_send, f1_recv, f2_send, f2_recv):
     rows, width = x_v.shape
@@ -86,16 +86,22 @@
 
     base = core * k_half
     direct_rows = k_half - SHARED_ROWS
-    sub_rows = SHARED_ROWS // ring
+    sub_cols = half // ring
+
+    def shared_rows(from_core):
+        return pl.ds(pl.multiple_of(from_core * k_half + direct_rows, 32), SHARED_ROWS)
 
     def sub_at(c, index):
-        return wox_v.at[c, pl.ds(pl.multiple_of(base + direct_rows + index * sub_rows, sub_rows), sub_rows), :]
+        return wox_v.at[c, shared_rows(core), pl.ds(pl.multiple_of(index * sub_cols, sub_cols), sub_cols)]
 
     def wo_part(c, kind):
-        start, count = (base, direct_rows) if kind == 0 else (base + direct_rows + chip * sub_rows, sub_rows)
-        ks = pl.ds(pl.multiple_of(start, sub_rows), count)
-        return remote(wo_hbm.at[ks, c * half:(c + 1) * half], wox_v.at[c, ks, :],
-                      wo_send.at[c, kind], wo_recv.at[c, kind], y_mate[c])
+        if kind:
+            src = wo_hbm.at[shared_rows(core), pl.ds(pl.multiple_of(c * half + chip * sub_cols, sub_cols), sub_cols)]
+            dst = sub_at(c, chip)
+        else:
+            ks = pl.ds(pl.multiple_of(base, 32), direct_rows)
+            src, dst = wo_hbm.at[ks, c * half:(c + 1) * half], wox_v.at[c, ks, :]
+        return remote(src, dst, wo_send.at[c, kind], wo_recv.at[c, kind], y_mate[c])
 
     def wx_own(d, c, index):
         return remote(sub_at(c, index), sub_at(c, index), wx_send.at[d, c], wx_recv.at[d, c], x_left if d else x_right)
@@ -104,8 +110,8 @@
         return remote(sub_at(c, index), sub_at(c, index), wf_send.at[d, c], wf_recv.at[d, c], x_left if d else x_right)
 
     def wo_share(c, kind, from_core):
-        start = from_core * k_half + kind * direct_rows
-        part = wox_v.at[c, pl.ds(pl.multiple_of(start, sub_rows), SHARED_ROWS if kind else direct_rows), :]
+        ks = shared_rows(from_core) if kind else pl.ds(pl.multiple_of(from_core * k_half, 32), direct_rows)
+        part = wox_v.at[c, ks, :]
         return remote(part, part, wo_fwd_send.at[c, kind], wo_fwd_recv.at[c, kind], sibling)
 
     chip_left, chip_right, chip_far = (chip + ring - 1) % ring, (chip + 1) % ring, (chip + 2) % ring
@@ -131,20 +137,26 @@
         return remote(kv_v.at[0, 0, head], kv_v.at[rel, cc, head],
                       kv_send.at[rel, head], kv_recv.at[rel, cc, head], peer)
 
-    def own_chunk(rel, head, peer, i):
-        ks = slice(i * chunk, (i + 1) * chunk)
+    def piece_sem(rel, head, late):
+        return late_recv.at[rel] if late else kv_recv.at[rel, 0, head]
+
+    def own_chunk(rel, head, peer, i, count=1, late=False):
+        ks = slice(i * chunk, (i + count) * chunk)
         return remote(kv_v.at[0, 0, head, :, ks, :], kv_v.at[rel, 0, head, :, ks, :],
-                      kv_send.at[rel, head], kv_recv.at[rel, 0, head], peer)
-
-    def left_v(head, ks=slice(None)):
+                      kv_send.at[rel, head], piece_sem(rel, head, late), peer)
+
+    def left_v(head, ks=slice(None), late=False):
         return remote(kv_v.at[0, 0, head, 1, ks, :], kv_v.at[2, 0, head, 1, ks, :],
-                      kv_send.at[2, head], kv_recv.at[2, 0, head], x_left)
-
-    def far_k(head):
-        return remote(kv_v.at[1, 0, head, 0], kv_v.at[3, 0, head, 0], far_send.at[head, 0], far_recv.at[head, 0], x_right)
-
-    def far_v(head):
-        return remote(kv_v.at[2, 0, head, 1], kv_v.at[3, 0, head, 1], far_send.at[head, 1], far_recv.at[head, 1], x_left)
+                      kv_send.at[2, head], piece_sem(2, head, late), x_left)
+
+    half_chunks = LOAD_CHUNKS // 2
+    key_halves = (slice(0, half_chunks * chunk), slice(half_chunks * chunk, rows))
+
+    def far_k(head, ks=slice(None)):
+        return remote(kv_v.at[1, 0, head, 0, ks, :], kv_v.at[3, 0, head, 0, ks, :], far_send.at[head, 0], far_recv.at[head, 0], x_right)
+
+    def far_v(head, ks=slice(None)):
+        return remote(kv_v.at[2, 0, head, 1, ks, :], kv_v.at[3, 0, head, 1, ks, :], far_send.at[head, 1], far_recv.at[head, 1], x_left)
 
     def fwd_sib(rel, head):
         return remote(kv_v.at[rel, 0, head], kv_v.at[rel, 1, head],
@@ -194,18 +206,20 @@
         own_to(0, 1, 0, sibling).start()
         own_to(0, 1, 1, sibling).start()
 
-    @pl.when(right_sends)
-    def _():
-        own_to(1, 0, 1, x_right).start()
-
-    @pl.when(chip == 0)
-    def _():
-        own_to(2, 0, 1, x_left).start()
-
-    @pl.when(chip == 1)
-    def _():
-        left_v(1).start()
-
+    def head_one(i):
+        @pl.when(right_sends)
+        def _():
+            own_chunk(1, 1, x_right, i * half_chunks, half_chunks, i == 1).start()
+
+        @pl.when(chip == 0)
+        def _():
+            own_chunk(2, 1, x_left, i * half_chunks, half_chunks, i == 1).start()
+
+        @pl.when(chip == 1)
+        def _():
+            left_v(1, key_halves[i], i == 1).start()
+
+    head_one(0)
     loads[2].wait()
 
     with jax.named_scope('q_proj'):
@@ -281,57 +295,81 @@
     has_far = chip >= 2
     fwd_right = jnp.logical_and(chip >= 1, chip <= 2)
 
-    def take_left(head):
-        own_to(1, 0, head, x_right).wait_recv()
-
-        @pl.when(fwd_right)
-        def _():
-            far_k(head).start()
-
-        fwd_sib(1, head).start()
-
-    def take_right(head):
-        own_to(2, 0, head, x_left).wait_recv()
-        far_v(head).start()
-        fwd_sib(2, head).start()
-
-    def relay_right(head):
-        left_v(head).wait_recv()
-        far_v(head).start()
+    def take_head_zero():
+        @pl.when(has_left)
+        def _():
+            own_to(1, 0, 0, x_right).wait_recv()
+
+            @pl.when(fwd_right)
+            def _():
+                far_k(0).start()
+
+            fwd_sib(1, 0).start()
+
+        @pl.when(has_right)
+        def _():
+            own_to(2, 0, 0, x_left).wait_recv()
+            far_v(0).start()
+            fwd_sib(2, 0).start()
+
+        @pl.when(chip == 0)
+        def _():
+            left_v(0).wait_recv()
+            far_v(0).start()
+
+    def take_head_one(i):
+        @pl.when(has_left)
+        def _():
+            own_chunk(1, 1, x_right, i * half_chunks, half_chunks, i == 1).wait_recv()
+
+            @pl.when(fwd_right)
+            def _():
+                far_k(1, key_halves[i]).start()
+
+            if i == 1:
+                fwd_sib(1, 1).start()
+
+        @pl.when(has_right)
+        def _():
+            own_chunk(2, 1, x_left, i * half_chunks, half_chunks, i == 1).wait_recv()
+            far_v(1, key_halves[i]).start()
+            if i == 1:
+                fwd_sib(2, 1).start()
+
+        @pl.when(chip == 0)
+        def _():
+            left_v(1, key_halves[i], i == 1).wait_recv()
+            far_v(1, key_halves[i]).start()
 
     @pl.when(core == 1)
     def _():
         own_to(0, 1, 0, sibling).wait_recv()
         own_to(0, 1, 1, sibling).wait_recv()
 
-    @pl.when(has_left)
-    def _():
-        take_left(0)
-
-    @pl.when(has_right)
-    def _():
-        take_right(0)
-
-    @pl.when(chip == 0)
-    def _():
-        relay_right(0)
+    take_head_zero()
+    head_one(1)
 
     ends = jnp.logical_or(chip == 0, chip == 3)
 
-    def wx_start(d):
-        for c in range(2):
-            wx_own(d, c, chip).start()
+    def wx_late(c):
+        @pl.when(fwd_right)
+        def _():
+            wx_own(0, c, chip).start()
+
+        @pl.when(ends)
+        def _():
+            wx_own(1, c, chip).start()
 
     for c in range(2):
         wo_part(c, 1).wait_recv()
 
-    @pl.when(ends)
-    def _():
-        wx_start(0)
-
-    @pl.when(fwd_right)
-    def _():
-        wx_start(1)
+        @pl.when(ends)
+        def _(c=c):
+            wx_own(0, c, chip).start()
+
+        @pl.when(fwd_right)
+        def _(c=c):
+            wx_own(1, c, chip).start()
 
     def sibling_unit(head, carry):
         far_unit(0, (1,), head)
@@ -340,14 +378,6 @@
     @pl.when(core == 1)
     def _():
         lax.fori_loop(0, kv_heads, sibling_unit, 0)
-
-    @pl.when(fwd_right)
-    def _():
-        take_left(1)
-
-    @pl.when(chip == 0)
-    def _():
-        relay_right(1)
 
     def seg(index):
         return pl.ds(pl.multiple_of(index * seg_rows, seg_rows), seg_rows)
@@ -371,56 +401,46 @@
     def sib_wait(rel, head):
         remote(kv_v.at[rel, 0, head], kv_v.at[rel, 1, head], kv_fwd_send.at[rel, head], kv_recv.at[rel, 1, head], sibling).wait_recv()
 
+    shift = (chip // (ring - 1)) * (1 - core)
+
     def side_unit(u, carry):
-        head = (1 - u % 2) * ((u + 2) // 4)
-        rel = (1 - u % 2) * (1 + u // 4) + (u % 2) * (2 + u // 3)
+        head = u // 3
+        rel = 1 + u % 3
         need = ((rel == 1) & has_left) | ((rel == 2) & has_right) | ((rel == 3) & has_far)
 
         @pl.when((u == 0) & has_left)
         def _():
             sib_wait(1, 0)
 
-        @pl.when((u == 1) & has_right)
-        def _():
-            take_left(1)
-            take_right(1)
-
-        @pl.when((u == 1) & fwd_right)
-        def _():
-            wx_start(0)
-
-        @pl.when((u == 1) & ends)
-        def _():
-            wx_start(1)
-
-        @pl.when((u == 1) & has_right)
-        def _():
-            sib_wait(2, 0)
-
-        @pl.when((u == 2) & (chip < 2))
-        def _():
-            with jax.named_scope('wx_wait'):
-                for d in range(2):
-                    for c in range(2):
-                        wx_own(d, c, chip_right if d else chip_left).wait_recv()
-                        wx_pass(d, c, chip_right if d else chip_left).start()
-
-        @pl.when((u == 2) & has_far)
+        at = u - shift
+
+        @pl.when((at == 1) & has_far)
         def _():
             with jax.named_scope('far_h0'):
                 far_k(0).wait_recv()
                 far_v(0).wait_recv()
                 fwd_sib(3, 0).start()
 
-        @pl.when((u == 2) & has_left)
-        def _():
-            sib_wait(1, 1)
-
-        @pl.when((u == 3) & has_far)
+        @pl.when((u == 1) & has_right)
+        def _():
+            sib_wait(2, 0)
+
+        @pl.when(u == 1)
+        def _():
+            take_head_one(0)
+
+        @pl.when(at == 2)
+        def _():
+            with jax.named_scope('take_h1'):
+                take_head_one(1)
+                for c in range(2):
+                    wx_late(c)
+
+        @pl.when((u == 2) & has_far)
         def _():
             sib_wait(3, 0)
 
-        @pl.when(u == 4)
+        @pl.when(u == 3)
         def _():
             finish_rows(0, slice(0, rows))
             for c in range(2):
@@ -428,16 +448,17 @@
             for c in range(2):
                 o_part(c, 1, 0).start()
 
-        @pl.when((u == 4) & has_far)
-        def _():
-            with jax.named_scope('far_h1'):
-                far_k(1).wait_recv()
-                far_v(1).wait_recv()
-                fwd_sib(3, 1).start()
-
-        @pl.when((u == 4) & has_right)
-        def _():
-            sib_wait(2, 1)
+        @pl.when((u == 3) & (chip < 2))
+        def _():
+            with jax.named_scope('wx_wait'):
+                for c in range(2):
+                    for d in range(2):
+                        wx_own(d, c, chip_right if d else chip_left).wait_recv()
+                        wx_pass(d, c, chip_right if d else chip_left).start()
+
+        @pl.when((u == 3) & has_left)
+        def _():
+            sib_wait(1, 1)
 
         @pl.when(need)
         def _():
@@ -445,25 +466,75 @@
 
         return carry
 
-    lax.fori_loop(0, 5, side_unit, 0)
-
-    with jax.named_scope('wo_wait'):
-        for c in range(2):
-            wo_part(c, 0).wait_recv()
-            wo_share(c, 0, core).start()
+    lax.fori_loop(0, 4, side_unit, 0)
+
+    @pl.when(has_far)
+    def _():
+        with jax.named_scope('far_h1'):
+            far_k(1).wait_recv()
+            far_v(1).wait_recv()
+            fwd_sib(3, 1).start()
 
     @pl.when(has_far)
     def _():
         sib_wait(3, 1)
 
+    @pl.when(has_right)
+    def _():
+        sib_wait(2, 1)
+
+    def col(c, g):
+        return pl.ds(pl.multiple_of(c * half + g * cols, cols), cols)
+
+    def two_mates(c, g, own_rows, which):
+        g0 = pl.multiple_of(g * cols, cols)
+        return (jnp.dot(o_v[seg(own_rows), :], wo_v[:, col(c, g)], preferred_element_type=F32)
+                + jnp.dot(ox_v[c, which], wox_v[c, :, pl.ds(g0, cols)], preferred_element_type=F32))
+
+    def cross(c, g):
+        return remote(part_v.at[c, g], recv_v.at[c, g], part_send.at[c, g], part_recv.at[c, g], y_mate[1 - c])
+
+    def f1(c, g, d, owner):
+        block = out_v.at[seg(owner), col(c, g)]
+        return remote(block, block, f1_send.at[c, g, d], f1_recv.at[c, g, d], y_left if d else y_right)
+
+    def f2(g, d, owner):
+        block = out_v.at[seg(owner), col(d, g)]
+        return remote(block, block, f2_send.at[g, d], f2_recv.at[g, d], y_left if d else y_right)
+
+    def project_cross(g, carry):
+        for c in range(2):
+            part_v[c, g] = two_mates(c, g, mate_seg[1 - c], 0).astype(BF)
+            cross(c, g).start()
+        return carry
+
     def seg_step(j, carry):
         index = (tp + ring + 2 * ((3 - j) // 3) + turn * ((j % 3) % 2) - turn * (j // 2 - j // 3)) % ring
         rs = seg(index)
 
-        @pl.when(has_far)
+        @pl.when(j == 3)
+        def _():
+            with jax.named_scope('mates'):
+                for c in range(2):
+                    for kind in range(2):
+                        wo_share(c, kind, 1 - core).wait_recv()
+                    for head in range(kv_heads):
+                        o_part(c, 0, head).wait_recv()
+            with jax.named_scope('cross'):
+                lax.fori_loop(0, CHUNKS, project_cross, 0)
+
+        def seg_tiles(*rels):
+            return [(rel, (0, 1), 1, group_size + g, rs, 0) for rel in rels for g in range(group_size)]
+
+        @pl.when(has_right)
         def _():
             with jax.named_scope('far_seg'):
-                attend([(3, (0, 1), 1, group_size + g, rs, 0) for g in range(group_size)], False)
+                attend(seg_tiles(2, 3), False)
+
+        @pl.when(has_far & (chip < 3))
+        def _():
+            with jax.named_scope('far_seg'):
+                attend(seg_tiles(3), False)
 
         finish_rows(1, rs)
 
@@ -471,14 +542,14 @@
         def _():
             for c in range(2):
                 o_part(c, 0, 1).start()
+            with jax.named_scope('wo_wait'):
+                for c in range(2):
+                    wo_part(c, 0).wait_recv()
+                    wo_share(c, 0, core).start()
 
         @pl.when(j == 1)
         def _():
             o_part(0, 1, 1).start()
-
-        @pl.when(j == 2)
-        def _():
-            o_part(1, 1, 1).start()
             with jax.named_scope('sub_wait'):
                 @pl.when(has_far)
                 def _():
@@ -495,45 +566,14 @@
                 for c in range(2):
                     wo_share(c, 1, core).start()
 
+        @pl.when(j == 2)
+        def _():
+            o_part(1, 1, 1).start()
+
         return carry
 
     with jax.named_scope('segs'):
         lax.fori_loop(0, ring, seg_step, 0)
-
-    def col(c, g):
-        return pl.ds(pl.multiple_of(c * half + g * cols, cols), cols)
-
-    def two_mates(c, g, own_rows, which):
-        g0 = pl.multiple_of(g * cols, cols)
-        return (jnp.dot(o_v[seg(own_rows), :], wo_v[:, col(c, g)], preferred_element_type=F32)
-                + jnp.dot(ox_v[c, which], wox_v[c, :, pl.ds(g0, cols)], preferred_element_type=F32))
-
-    def cross(c, g):
-        return remote(part_v.at[c, g], recv_v.at[c, g], part_send.at[c, g], part_recv.at[c, g], y_mate[1 - c])
-
-    def f1(c, g, d, owner):
-        block = out_v.at[seg(owner), col(c, g)]
-        return remote(block, block, f1_send.at[c, g, d], f1_recv.at[c, g, d], y_left if d else y_right)
-
-    def f2(g, d, owner):
-        block = out_v.at[seg(owner), col(d, g)]
-        return remote(block, block, f2_send.at[g, d], f2_recv.at[g, d], y_left if d else y_right)
-
-    with jax.named_scope('mates'):
-        for c in range(2):
-            for kind in range(2):
-                wo_share(c, kind, 1 - core).wait_recv()
-            for head in range(kv_heads):
-                o_part(c, 0, head).wait_recv()
-
-    def project_cross(g, carry):
-        for c in range(2):
-            part_v[c, g] = two_mates(c, g, mate_seg[1 - c], 0).astype(BF)
-            cross(c, g).start()
-        return carry
-
-    with jax.named_scope('cross'):
-        lax.fori_loop(0, CHUNKS, project_cross, 0)
 
     with jax.named_scope('caches'):
         k_out[...] = kc_v[...].reshape(k_out.shape)
@@ -680,7 +720,7 @@
                 dma((3, kv_heads)),
                 dma((4, 2, kv_heads)),
                 dma((4, kv_heads)),
-                dma((kv_heads, 2)), dma((kv_heads, 2)),
+                dma((kv_heads, 2)), dma((kv_heads, 2)), dma((3,)),
                 dma((2, 2)), dma((2, 2)), dma((2, 2)), dma((2, 2)), dma((2, 2)), dma((2, 2)), dma((2, 2)), dma((2, 2)),
                 dma((2, 2, kv_heads)), dma((2, 2, kv_heads)),
                 dma((2, CHUNKS)), dma((2, CHUNKS)),

time: 78.4 us -> 77.1 us (0.983)
  Pallas kernels: 74 us -> 73.2 us
where the time goes in v6:
time: 77.1 us; the launch traced here: 77 us
  Pallas kernels  73.2 us (95%)
  local copies, waits for them, and re-layouts  3.07 us (4%)
    pallas_call x1, Pallas kernels, local_block(): pl.pallas_call(lambda *refs: block_kernel(ring, kv_heads, q_heads // kv_h...  73.2 us
    unnamed x3, local copies, waits for them, and re-layouts  3.07 us

profile of v6, /device:TPU:102, one launch (start us, length us, event | category | flops | bytes accessed | tf_op | source)
XLA Modules:
  0.0 77.0 jit_solution(16273507782928657845)
XLA Ops:
  0.6 73.2 %attn_block.1 = (bf16[512,3072]{1,0:T(8,128)(2,1)S(1)}, bf16[512,2,128]{2,1,0:T(2,128)(2,1)S(1)}, bf16[512,2,128]{2,1,0:T(2,128)(2,1)S(1)}) custom-call(bf16[512,3072]{1,0:T(8,128)(2,1)} %refs_0_.1, s32[512]{0:T(512)} %refs_1_.1, bf16[3072]{0:T(1024)(128)(2,1)} %refs_2_.1, f32[1,128]{1,0:T(1,128)} %constant.2.clone.refs_3_, bf16[3072,768]{1,0:T(8,128)(2,1)} %refs_4_.1, ...), custom_call_target="tpu_custom_call" | custom-call | tf_op jit(solution)/shard_map/attn_block/pallas_call | solution.py:689
  73.9 1.7 %copy.14 = bf16[512,3072]{1,0:T(8,128)(2,1)} copy(bf16[512,3072]{1,0:T(8,128)(2,1)S(1)} %get-tuple-element.3) | data formatting | bytes 6291456
  75.6 0.7 copy.15
  76.3 0.7 copy.16

commit v7 on v6

--- a/solution.py
+++ b/solution.py
@@ -26,9 +26,9 @@
 
 
 def block_kernel(ring, kv_heads, group_size,
-                 x_hbm, pos_ref, gain_ref, freq_ref, wq_hbm, wk_hbm, wv_hbm, wo_hbm,
+                 x_hbm, pos_hbm, gain_hbm, freq_hbm, wq_hbm, wk_hbm, wv_hbm, wo_hbm,
                  out_v, k_out, v_out,
-                 x_v, h_v, wq_v, wkv_v, wo_v, cos_v, sin_v, kc_v, vc_v, q_v, kv_v, m_v, l_v, acc_v, o_v,
+                 pos_ref, gain_ref, freq_ref, x_v, h_v, wq_v, wkv_v, wo_v, cos_v, sin_v, kc_v, vc_v, q_v, kv_v, m_v, l_v, acc_v, o_v,
                  wox_v, ox_v, part_v, recv_v,
                  load_sem, kv_send, kv_recv, kv_fwd_send, far_send, far_recv, late_recv,
                  wo_send, wo_recv, wx_send, wx_recv, wf_send, wf_recv, wo_fwd_send, wo_fwd_recv, o_send, o_recv, part_send, part_recv,
@@ -51,31 +51,42 @@
     turn = 1 - 2 * (tp % 2)
     y_mate = ({'tp': (tp + ring + turn) % ring}, {'tp': (tp + ring - turn) % ring})
 
+    barrier = pltpu.get_barrier_semaphore()
+    for peer in (x_right, x_left, sibling, y_right, y_left):
+        pl.semaphore_signal(barrier, inc=1, device_id=peer, device_id_type=pl.DeviceIdType.MESH)
+
     kv_cols = kv_heads * HEAD
     chunk = rows // LOAD_CHUNKS
     x_loads = [pltpu.make_async_copy(x_hbm.at[i * chunk:(i + 1) * chunk, :], x_v.at[i * chunk:(i + 1) * chunk, :],
                                      load_sem.at[4 + i]) for i in range(LOAD_CHUNKS)]
     loads = [
-        pltpu.make_async_copy(wk_hbm, wkv_v.at[:, :kv_cols], load_sem.at[0]),
-        pltpu.make_async_copy(wv_hbm, wkv_v.at[:, kv_cols:], load_sem.at[1]),
+        pltpu.make_async_copy(wk_hbm, wkv_v.at[0], load_sem.at[0]),
+        pltpu.make_async_copy(wv_hbm, wkv_v.at[1], load_sem.at[1]),
         pltpu.make_async_copy(wq_hbm, wq_v, load_sem.at[2]),
         pltpu.make_async_copy(wo_hbm, wo_v, load_sem.at[3]),
     ]
-    for copy in x_loads[:1] + loads[:2] + x_loads[1:] + loads[2:3]:
+    small = [pltpu.make_async_copy(src, dst, load_sem.at[4 + LOAD_CHUNKS + i])
+             for i, (src, dst) in enumerate(((pos_hbm, pos_ref), (freq_hbm, freq_ref), (gain_hbm, gain_ref)))]
+    for copy in small + x_loads[:1] + loads[:2] + x_loads[1:]:
         copy.start()
 
-    barrier = pltpu.get_barrier_semaphore()
-    for peer in (x_right, x_left, sibling, y_right, y_left):
-        pl.semaphore_signal(barrier, inc=1, device_id=peer, device_id_type=pl.DeviceIdType.MESH)
-
     with jax.named_scope('load_wait'):
+        for copy in small:
+            copy.wait()
         pos = pos_ref[...].astype(F32).reshape(rows // HEAD, HEAD)
         pos = jnp.concatenate([pos, jnp.zeros((8 - rows // HEAD, HEAD), F32)], axis=0).T
-        sign = jnp.where(lax.broadcasted_iota(jnp.int32, (1, HEAD), 1) < HEAD // 2, -1.0, 1.0)
-        for i in range(rows // HEAD):
-            angles = pos[:, i:i + 1] * freq_ref[...]
-            cos_v[i * HEAD:(i + 1) * HEAD, :] = jnp.cos(angles)
-            sin_v[i * HEAD:(i + 1) * HEAD, :] = jnp.sin(angles) * sign
+        first = lax.broadcasted_iota(jnp.int32, (1, HEAD), 1) < HEAD // 2
+        def tables(i):
+            k = i + rows // HEAD // 2
+            angles = jnp.where(first, pos[:, i:i + 1], pos[:, k:k + 1]) * freq_ref[...]
+            cos_t, sin_t = jnp.cos(angles), jnp.sin(angles)
+            cos_r, sin_r = pltpu.roll(cos_t, HEAD // 2, 1), pltpu.roll(sin_t, HEAD // 2, 1)
+            for row, lo_c, hi_c, lo_s, hi_s in ((i, cos_t, cos_r, sin_t, sin_r), (k, cos_r, cos_t, sin_r, sin_t)):
+                cos_v[row * HEAD:(row + 1) * HEAD, :] = jnp.where(first, lo_c, hi_c)
+                sin_v[row * HEAD:(row + 1) * HEAD, :] = jnp.where(first, -lo_s, hi_s)
+
+        for i in range(rows // HEAD // 2):
+            tables(i)
 
     def remote(src, dst, send, recv, peer):
         return pltpu.make_async_remote_copy(src_ref=src, dst_ref=dst, send_sem=send, recv_sem=recv,
@@ -167,37 +178,40 @@
     x_loads[0].wait()
     with jax.named_scope('norm'):
         lax.fori_loop(0, chunk // NORM_ROWS, norm_step, 0)
+    loads[2].start()
     for copy in loads[:2]:
         copy.wait()
-    for i in range(LOAD_CHUNKS):
-        if i + 1 < LOAD_CHUNKS:
-            x_loads[i + 1].wait()
-        ks = slice(i * chunk, (i + 1) * chunk)
+    steps = ((0, 1), (1, 1), (2, LOAD_CHUNKS - 2))
+    for n, (i, count) in enumerate(steps):
+        ahead = steps[n + 1] if n + 1 < len(steps) else (0, 0)
+        for k in range(ahead[0], sum(ahead)):
+            x_loads[k].wait()
+        ks = slice(i * chunk, (i + count) * chunk)
         with jax.named_scope('kv_proj'):
-            kv_proj = jnp.dot(h_v[ks, :], wkv_v[...], preferred_element_type=F32)
-            if i + 1 < LOAD_CHUNKS:
-                for r in range(0, chunk, 16):
-                    norm_rows((i + 1) * chunk + r, 16)
+            k_proj, v_proj = (jnp.dot(h_v[ks, :], wkv_v[w], preferred_element_type=F32) for w in range(2))
+            for r in range(ahead[0] * chunk, sum(ahead) * chunk, 16):
+                norm_rows(r, 16)
             for h in range(kv_heads):
                 hc = slice(h * HEAD, (h + 1) * HEAD)
-                k_head = rope(kv_proj[:, hc], ks)
+                k_head = rope(k_proj[:, hc], ks)
                 kv_v[0, 0, h, 0, ks, :] = k_head
                 kc_v[ks, hc] = k_head
-                v_head = kv_proj[:, kv_cols + h * HEAD:kv_cols + (h + 1) * HEAD].astype(BF)
+                v_head = v_proj[:, hc].astype(BF)
                 vc_v[ks, hc] = v_head
-                kv_v[0, 0, h, 1, ks, :] = v_head.T
+                for k in range(count):
+                    kv_v[0, 0, h, 1, (i + k) * chunk:(i + k + 1) * chunk, :] = v_head[k * chunk:(k + 1) * chunk, :].T
 
         @pl.when(right_sends)
-        def _(i=i):
-            own_chunk(1, 0, x_right, i).start()
+        def _(i=i, count=count):
+            own_chunk(1, 0, x_right, i, count).start()
 
         @pl.when(chip == 0)
-        def _(i=i):
-            own_chunk(2, 0, x_left, i).start()
+        def _(i=i, count=count):
+            own_chunk(2, 0, x_left, i, count).start()
 
         @pl.when(chip == 1)
-        def _(i=i):
-            left_v(0, slice(i * chunk, (i + 1) * chunk)).start()
+        def _(ks=ks):
+            left_v(0, ks).start()
 
     loads[3].start()
 
@@ -475,10 +489,6 @@
             far_v(1).wait_recv()
             fwd_sib(3, 1).start()
 
-    @pl.when(has_far)
-    def _():
-        sib_wait(3, 1)
-
     @pl.when(has_right)
     def _():
         sib_wait(2, 1)
@@ -528,10 +538,14 @@
 
         @pl.when(has_right)
         def _():
-            with jax.named_scope('far_seg'):
-                attend(seg_tiles(2, 3), False)
-
-        @pl.when(has_far & (chip < 3))
+            with jax.named_scope('right_seg'):
+                attend(seg_tiles(2), False)
+
+        @pl.when((j == 0) & has_far)
+        def _():
+            sib_wait(3, 1)
+
+        @pl.when(has_far)
         def _():
             with jax.named_scope('far_seg'):
                 attend(seg_tiles(3), False)
@@ -669,6 +683,16 @@
             @pl.when(sent)
             def _(rel=rel, head=head):
                 fwd_sib(rel, head).wait_send()
+
+
+def copy_out(*refs):
+    count = len(refs) // 2
+    sems = refs[-1]
+    copies = [pltpu.make_async_copy(refs[i], refs[count + i], sems.at[i]) for i in range(count)]
+    for copy in copies:
+        copy.start()
+    for copy in copies:
+        copy.wait()
 
 
 def solution(mesh):
@@ -693,14 +717,16 @@
                 pltpu.VMEM((rows, kv_heads, HEAD), BF),
                 pltpu.VMEM((rows, kv_heads, HEAD), BF),
             ),
-            in_specs=[pl.BlockSpec(memory_space=pl.ANY)] + [pl.BlockSpec(memory_space=pltpu.VMEM)] * 3
-            + [pl.BlockSpec(memory_space=pl.ANY)] * 4,
+            in_specs=[pl.BlockSpec(memory_space=pl.ANY)] * 8,
             out_specs=[pl.BlockSpec(memory_space=pltpu.VMEM)] * 3,
             scratch_shapes=[
+                pltpu.VMEM((rows,), jnp.int32),
+                pltpu.VMEM((width,), BF),
+                pltpu.VMEM((1, HEAD), F32),
                 pltpu.VMEM((rows, width), BF),
                 pltpu.VMEM((rows, width), BF),
                 pltpu.VMEM(w_query.shape, BF),
-                pltpu.VMEM((width, 2 * kv_heads * HEAD), BF),
+                pltpu.VMEM((2, width, kv_heads * HEAD), BF),
                 pltpu.VMEM(w_out.shape, BF),
                 pltpu.VMEM((rows, HEAD), F32),
                 pltpu.VMEM((rows, HEAD), F32),
@@ -716,7 +742,7 @@
                 pltpu.VMEM((2, 2, seg_rows, q_heads * HEAD), BF),
                 pltpu.VMEM((2, CHUNKS, seg_rows, cols), BF),
                 pltpu.VMEM((2, CHUNKS, seg_rows, cols), BF),
-                dma((4 + LOAD_CHUNKS,)),
+                dma((7 + LOAD_CHUNKS,)),
                 dma((3, kv_heads)),
                 dma((4, 2, kv_heads)),
                 dma((4, kv_heads)),
@@ -730,7 +756,16 @@
             compiler_params=pltpu.CompilerParams(collective_id=0, has_side_effects=True, vmem_limit_bytes=60 * 1024 * 1024),
             name='attn_block',
         )(hidden, positions, norm_gain, jnp.asarray(inverse_freq()), w_query, w_key, w_value, w_out)
-        return out, k_new, v_new
+        results = [pltpu.with_memory_space_constraint(r, pltpu.VMEM) for r in (out, k_new, v_new)]
+        return pl.pallas_call(
+            copy_out,
+            out_shape=tuple(jax.ShapeDtypeStruct(r.shape, r.dtype) for r in results),
+            in_specs=[pl.BlockSpec(memory_space=pltpu.VMEM)] * 3,
+            out_specs=[pl.BlockSpec(memory_space=pl.ANY)] * 3,
+            scratch_shapes=[dma((3,))],
+            compiler_params=pltpu.CompilerParams(vmem_limit_bytes=8 * 1024 * 1024),
+            name='copy_out',
+        )(*results)
 
     return jax.shard_map(local_block, mesh=mesh,
                          in_specs=(row_spec, P(('dp', 'cp')), P(None), head_cols, head_cols, head_cols, P('tp', None)),

time: 77.1 us -> 75.6 us (0.981)
  local copies, waits for them, and re-layouts: 3.07 us -> 0 us
  Pallas kernels: 73.2 us -> 74.7 us
    unnamed x3 -> x0, local copies, waits for them, and re-layouts: 3.07 us -> none
    pallas_call x0 -> x1, Pallas kernels: none -> 1.85 us  [local_block(): pl.pallas_call(copy_out, out_shape=tuple((jax.ShapeDtypeStruct(r.shape, r...]
where the time goes in v7:
time: 75.6 us; the launch traced here: 75.5 us
  Pallas kernels  74.7 us (99%)
  between operations  0.8 us (1%)
    pallas_call x1, Pallas kernels, local_block(): pl.pallas_call(lambda *refs: block_kernel(ring, kv_heads, q_heads // kv_h...  72.8 us
    pallas_call x1, Pallas kernels, local_block(): pl.pallas_call(copy_out, out_shape=tuple((jax.ShapeDtypeStruct(r.shape, r...  1.85 us

profile of v7, /device:TPU:102, one launch (start us, length us, event | category | flops | bytes accessed | tf_op | source)
XLA Modules:
  0.0 75.5 jit_solution(8722886390758557806)
XLA Ops:
  0.6 72.8 %attn_block.1 = (bf16[512,3072]{1,0:T(8,128)(2,1)S(1)}, bf16[512,2,128]{2,1,0:T(2,128)(2,1)S(1)}, bf16[512,2,128]{2,1,0:T(2,128)(2,1)S(1)}) custom-call(bf16[512,3072]{1,0:T(8,128)(2,1)} %refs_0_.1, s32[512]{0:T(512)} %refs_1_.1, bf16[3072]{0:T(1024)(128)(2,1)} %refs_2_.1, f32[1,128]{1,0:T(1,128)} %constant.2.clone.refs_3_, bf16[3072,768]{1,0:T(8,128)(2,1)} %refs_4_.1, ...), custom_call_target="tpu_custom_call" | custom-call | tf_op jit(solution)/shard_map/attn_block/pallas_call | solution.py:713
  73.5 1.9 %copy_out.1 = (bf16[512,3072]{1,0:T(8,128)(2,1)}, bf16[512,2,128]{2,1,0:T(2,128)(2,1)}, bf16[512,2,128]{2,1,0:T(2,128)(2,1)}) custom-call(bf16[512,3072]{1,0:T(8,128)(2,1)S(1)} %get-tuple-element.6.refs_0_, bf16[512,2,128]{2,1,0:T(2,128)(2,1)S(1)} %get-tuple-element.7.refs_1_, bf16[512,2,128]{2,1,0:T(2,128)(2,1)S(1)} %get-tuple-element.8.refs_2_), custom_call_target="tpu_custom_call" | custom-call | tf_op jit(solution)/shard_map/copy_out/pallas_call | solution.py:760

commit v8 on v7

--- a/solution.py
+++ b/solution.py
@@ -120,10 +120,13 @@
     def wx_pass(d, c, index):
         return remote(sub_at(c, index), sub_at(c, index), wf_send.at[d, c], wf_recv.at[d, c], x_left if d else x_right)
 
+    def all_bytes(ref, send, recv):
+        return remote(ref, ref, send, recv, sibling)
+
     def wo_share(c, kind, from_core):
         ks = shared_rows(from_core) if kind else pl.ds(pl.multiple_of(from_core * k_half, 32), direct_rows)
         part = wox_v.at[c, ks, :]
-        return remote(part, part, wo_fwd_send.at[c, kind], wo_fwd_recv.at[c, kind], sibling)
+        return remote(part, part, wo_fwd_send, wo_fwd_recv, sibling)
 
     chip_left, chip_right, chip_far = (chip + ring - 1) % ring, (chip + 1) % ring, (chip + 2) % ring
 
@@ -404,7 +407,7 @@
     def o_part(c, which, head):
         hc = slice(head * head_cols, (head + 1) * head_cols)
         return remote(o_v.at[seg(mate_seg[c] if which else far_seg), hc], ox_v.at[c, which, :, hc],
-                      o_send.at[c, which, head], o_recv.at[c, which, head], y_mate[c])
+                      o_send, o_recv.at[which], y_mate[c])
 
     def finish_rows(head, rs):
         for qi in range(head * group_size, (head + 1) * group_size):
@@ -502,15 +505,15 @@
                 + jnp.dot(ox_v[c, which], wox_v[c, :, pl.ds(g0, cols)], preferred_element_type=F32))
 
     def cross(c, g):
-        return remote(part_v.at[c, g], recv_v.at[c, g], part_send.at[c, g], part_recv.at[c, g], y_mate[1 - c])
+        return remote(part_v.at[c, g], recv_v.at[c, g], part_send, part_recv.at[c, g], y_mate[1 - c])
 
     def f1(c, g, d, owner):
         block = out_v.at[seg(owner), col(c, g)]
-        return remote(block, block, f1_send.at[c, g, d], f1_recv.at[c, g, d], y_left if d else y_right)
+        return remote(block, block, f1_send, f1_recv.at[c, g, d], y_left if d else y_right)
 
     def f2(g, d, owner):
         block = out_v.at[seg(owner), col(d, g)]
-        return remote(block, block, f2_send.at[g, d], f2_recv.at[g, d], y_left if d else y_right)
+        return remote(block, block, f2_send, f2_recv, y_left if d else y_right)
 
     def project_cross(g, carry):
         for c in range(2):
@@ -525,11 +528,9 @@
         @pl.when(j == 3)
         def _():
             with jax.named_scope('mates'):
-                for c in range(2):
-                    for kind in range(2):
-                        wo_share(c, kind, 1 - core).wait_recv()
-                    for head in range(kv_heads):
-                        o_part(c, 0, head).wait_recv()
+                all_bytes(wox_v.at[:, :k_half, :], wo_fwd_send, wo_fwd_recv).wait_recv()
+                all_bytes(ox_v.at[:, 0], o_send, o_recv.at[0]).wait_recv()
+
             with jax.named_scope('cross'):
                 lax.fori_loop(0, CHUNKS, project_cross, 0)
 
@@ -593,9 +594,7 @@
         k_out[...] = kc_v[...].reshape(k_out.shape)
         v_out[...] = vc_v[...].reshape(v_out.shape)
 
-    for c in range(2):
-        for head in range(kv_heads):
-            o_part(c, 1, head).wait_recv()
+    all_bytes(ox_v.at[:, 1], o_send, o_recv.at[1]).wait_recv()
 
     def project_own(g, carry):
         for c in range(2):
@@ -624,22 +623,19 @@
     def finish(g, carry):
         for d in range(2):
             f1(1 - d, g, d, side_seg[d]).wait_recv()
-            f2(g, d, far_seg).wait_recv()
         return carry
 
     with jax.named_scope('finish'):
         lax.fori_loop(0, CHUNKS, finish, 0)
 
-    def drain(g, carry):
-        for d in range(2):
-            cross(d, g).wait_send()
-            f2(g, d, side_seg[d]).wait_send()
-            for c in range(2):
-                f1(c, g, d, own_seg).wait_send()
-        return carry
-
     with jax.named_scope('drain'):
-        lax.fori_loop(0, CHUNKS, drain, 0)
+        own_rows = out_v.at[:seg_rows, :]
+        all_bytes(own_rows, f2_send, f2_recv).wait_recv()
+        all_bytes(own_rows, f2_send, f2_recv).wait_send()
+        all_bytes(out_v.at[:2 * seg_rows, :], f1_send, f2_recv).wait_send()
+        all_bytes(part_v, part_send, f2_recv).wait_send()
+        all_bytes(ox_v, o_send, f2_recv).wait_send()
+        all_bytes(wox_v.at[:, :k_half, :], wo_fwd_send, f2_recv).wait_send()
     for c in range(2):
         @pl.when(chip < 2)
         def _(c=c):
@@ -649,9 +645,6 @@
         for i in range(2):
             wo_part(c, i).wait_send()
             wx_own(i, c, chip).wait_send()
-            wo_share(c, i, core).wait_send()
-            for head in range(kv_heads):
-                o_part(c, i, head).wait_send()
 
     @pl.when(core == 0)
     def _():
@@ -747,11 +740,11 @@
                 dma((4, 2, kv_heads)),
                 dma((4, kv_heads)),
                 dma((kv_heads, 2)), dma((kv_heads, 2)), dma((3,)),
-                dma((2, 2)), dma((2, 2)), dma((2, 2)), dma((2, 2)), dma((2, 2)), dma((2, 2)), dma((2, 2)), dma((2, 2)),
-                dma((2, 2, kv_heads)), dma((2, 2, kv_heads)),
-                dma((2, CHUNKS)), dma((2, CHUNKS)),
-                dma((2, CHUNKS, 2)), dma((2, CHUNKS, 2)),
-                dma((CHUNKS, 2)), dma((CHUNKS, 2)),
+                dma((2, 2)), dma((2, 2)), dma((2, 2)), dma((2, 2)), dma((2, 2)), dma((2, 2)), dma(()), dma(()),
+                dma(()), dma((2,)),
+                dma(()), dma((2, CHUNKS)),
+                dma(()), dma((2, CHUNKS, 2)),
+                dma(()), dma(()),
             ],
             compiler_params=pltpu.CompilerParams(collective_id=0, has_side_effects=True, vmem_limit_bytes=60 * 1024 * 1024),
             name='attn_block',

time: 75.6 us -> 75.1 us (level)
  no operation moved by 1% of the time
where the time goes in v8:
time: 75.1 us; the launch traced here: 75 us
  Pallas kernels  74.2 us (99%)
  between operations  0.8 us (1%)
    pallas_call x1, Pallas kernels, local_block(): pl.pallas_call(lambda *refs: block_kernel(ring, kv_heads, q_heads // kv_h...  72.4 us
    pallas_call x1, Pallas kernels, local_block(): pl.pallas_call(copy_out, out_shape=tuple((jax.ShapeDtypeStruct(r.shape, r...  1.85 us

profile of v8, /device:TPU:102, one launch (start us, length us, event | category | flops | bytes accessed | tf_op | source)
XLA Modules:
  0.0 75.0 jit_solution(8987290563012436919)
XLA Ops:
  0.6 72.4 %attn_block.1 = (bf16[512,3072]{1,0:T(8,128)(2,1)S(1)}, bf16[512,2,128]{2,1,0:T(2,128)(2,1)S(1)}, bf16[512,2,128]{2,1,0:T(2,128)(2,1)S(1)}) custom-call(bf16[512,3072]{1,0:T(8,128)(2,1)} %refs_0_.1, s32[512]{0:T(512)} %refs_1_.1, bf16[3072]{0:T(1024)(128)(2,1)} %refs_2_.1, f32[1,128]{1,0:T(1,128)} %constant.2.clone.refs_3_, bf16[3072,768]{1,0:T(8,128)(2,1)} %refs_4_.1, ...), custom_call_target="tpu_custom_call" | custom-call | tf_op jit(solution)/shard_map/attn_block/pallas_call | solution.py:706
  73.0 1.9 %copy_out.1 = (bf16[512,3072]{1,0:T(8,128)(2,1)}, bf16[512,2,128]{2,1,0:T(2,128)(2,1)}, bf16[512,2,128]{2,1,0:T(2,128)(2,1)}) custom-call(bf16[512,3072]{1,0:T(8,128)(2,1)S(1)} %get-tuple-element.6.refs_0_, bf16[512,2,128]{2,1,0:T(2,128)(2,1)S(1)} %get-tuple-element.7.refs_1_, bf16[512,2,128]{2,1,0:T(2,128)(2,1)S(1)} %get-tuple-element.8.refs_2_), custom_call_target="tpu_custom_call" | custom-call | tf_op jit(solution)/shard_map/copy_out/pallas_call | solution.py:753

commit v9 on v8

--- a/solution.py
+++ b/solution.py
@@ -32,7 +32,7 @@
                  wox_v, ox_v, part_v, recv_v,
                  load_sem, kv_send, kv_recv, kv_fwd_send, far_send, far_recv, late_recv,
                  wo_send, wo_recv, wx_send, wx_recv, wf_send, wf_recv, wo_fwd_send, wo_fwd_recv, o_send, o_recv, part_send, part_recv,
-                 f1_send, f1_recv, f2_send, f2_recv):
+                 f1_send, f1_recv, f1_late, f2_send, f2_recv):
     rows, width = x_v.shape
     cp = lax.axis_index('cp')
     tp = lax.axis_index('tp')
@@ -112,13 +112,13 @@
         else:
             ks = pl.ds(pl.multiple_of(base, 32), direct_rows)
             src, dst = wo_hbm.at[ks, c * half:(c + 1) * half], wox_v.at[c, ks, :]
-        return remote(src, dst, wo_send.at[c, kind], wo_recv.at[c, kind], y_mate[c])
+        return remote(src, dst, wo_send, wo_recv.at[c, kind], y_mate[c])
 
     def wx_own(d, c, index):
-        return remote(sub_at(c, index), sub_at(c, index), wx_send.at[d, c], wx_recv.at[d, c], x_left if d else x_right)
+        return remote(sub_at(c, index), sub_at(c, index), wx_send, wx_recv.at[d, c], x_left if d else x_right)
 
     def wx_pass(d, c, index):
-        return remote(sub_at(c, index), sub_at(c, index), wf_send.at[d, c], wf_recv.at[d, c], x_left if d else x_right)
+        return remote(sub_at(c, index), sub_at(c, index), wf_send, wf_recv.at[d, c], x_left if d else x_right)
 
     def all_bytes(ref, send, recv):
         return remote(ref, ref, send, recv, sibling)
@@ -509,7 +509,7 @@
 
     def f1(c, g, d, owner):
         block = out_v.at[seg(owner), col(c, g)]
-        return remote(block, block, f1_send, f1_recv.at[c, g, d], y_left if d else y_right)
+        return remote(block, block, f1_send, f1_recv.at[c, g] if c == d else f1_late, y_left if d else y_right)
 
     def f2(g, d, owner):
         block = out_v.at[seg(owner), col(d, g)]
@@ -620,31 +620,22 @@
     with jax.named_scope('pass_on'):
         lax.fori_loop(0, CHUNKS, pass_on, 0)
 
-    def finish(g, carry):
-        for d in range(2):
-            f1(1 - d, g, d, side_seg[d]).wait_recv()
-        return carry
-
-    with jax.named_scope('finish'):
-        lax.fori_loop(0, CHUNKS, finish, 0)
-
     with jax.named_scope('drain'):
         own_rows = out_v.at[:seg_rows, :]
+        all_bytes(own_rows, f2_send, f1_late).wait_recv()
         all_bytes(own_rows, f2_send, f2_recv).wait_recv()
         all_bytes(own_rows, f2_send, f2_recv).wait_send()
         all_bytes(out_v.at[:2 * seg_rows, :], f1_send, f2_recv).wait_send()
         all_bytes(part_v, part_send, f2_recv).wait_send()
         all_bytes(ox_v, o_send, f2_recv).wait_send()
         all_bytes(wox_v.at[:, :k_half, :], wo_fwd_send, f2_recv).wait_send()
-    for c in range(2):
-        @pl.when(chip < 2)
-        def _(c=c):
-            for d in range(2):
-                wx_pass(d, c, chip_right if d else chip_left).wait_send()
-
-        for i in range(2):
-            wo_part(c, i).wait_send()
-            wx_own(i, c, chip).wait_send()
+    passed = wox_v.at[0, :SHARED_ROWS, :]
+    all_bytes(passed, wx_send, f2_recv).wait_send()
+    all_bytes(wox_v.at[0, :2 * (direct_rows + SHARED_ROWS // ring), :], wo_send, f2_recv).wait_send()
+
+    @pl.when(chip < 2)
+    def _():
+        all_bytes(passed, wf_send, f2_recv).wait_send()
 
     @pl.when(core == 0)
     def _():
@@ -740,10 +731,10 @@
                 dma((4, 2, kv_heads)),
                 dma((4, kv_heads)),
                 dma((kv_heads, 2)), dma((kv_heads, 2)), dma((3,)),
-                dma((2, 2)), dma((2, 2)), dma((2, 2)), dma((2, 2)), dma((2, 2)), dma((2, 2)), dma(()), dma(()),
+                dma(()), dma((2, 2)), dma(()), dma((2, 2)), dma(()), dma((2, 2)), dma(()), dma(()),
                 dma(()), dma((2,)),
                 dma(()), dma((2, CHUNKS)),
-                dma(()), dma((2, CHUNKS, 2)),
+                dma(()), dma((2, CHUNKS)), dma(()),
                 dma(()), dma(()),
             ],
             compiler_params=pltpu.CompilerParams(collective_id=0, has_side_effects=True, vmem_limit_bytes=60 * 1024 * 1024),

time: 75.1 us -> 75 us (level)
  no operation moved by 1% of the time
where the time goes in v9:
time: 75 us; the launch traced here: 74.9 us
  Pallas kernels  74.1 us (99%)
  between operations  0.8 us (1%)
    pallas_call x1, Pallas kernels, local_block(): pl.pallas_call(lambda *refs: block_kernel(ring, kv_heads, q_heads // kv_h...  72.2 us
    pallas_call x1, Pallas kernels, local_block(): pl.pallas_call(copy_out, out_shape=tuple((jax.ShapeDtypeStruct(r.shape, r...  1.85 us

profile of v9, /device:TPU:102, one launch (start us, length us, event | category | flops | bytes accessed | tf_op | source)
XLA Modules:
  0.0 74.9 jit_solution(14337402544221657943)
XLA Ops:
  0.6 72.2 %attn_block.1 = (bf16[512,3072]{1,0:T(8,128)(2,1)S(1)}, bf16[512,2,128]{2,1,0:T(2,128)(2,1)S(1)}, bf16[512,2,128]{2,1,0:T(2,128)(2,1)S(1)}) custom-call(bf16[512,3072]{1,0:T(8,128)(2,1)} %refs_0_.1, s32[512]{0:T(512)} %refs_1_.1, bf16[3072]{0:T(1024)(128)(2,1)} %refs_2_.1, f32[1,128]{1,0:T(1,128)} %constant.2.clone.refs_3_, bf16[3072,768]{1,0:T(8,128)(2,1)} %refs_4_.1, ...), custom_call_target="tpu_custom_call" | custom-call | tf_op jit(solution)/shard_map/attn_block/pallas_call | solution.py:697
  72.9 1.9 %copy_out.1 = (bf16[512,3072]{1,0:T(8,128)(2,1)}, bf16[512,2,128]{2,1,0:T(2,128)(2,1)}, bf16[512,2,128]{2,1,0:T(2,128)(2,1)}) custom-call(bf16[512,3072]{1,0:T(8,128)(2,1)S(1)} %get-tuple-element.6.refs_0_, bf16[512,2,128]{2,1,0:T(2,128)(2,1)S(1)} %get-tuple-element.7.refs_1_, bf16[512,2,128]{2,1,0:T(2,128)(2,1)S(1)} %get-tuple-element.8.refs_2_), custom_call_target="tpu_custom_call" | custom-call | tf_op jit(solution)/shard_map/copy_out/pallas_call | solution.py:744
